TPU v7x, 256 devices: a whole 4x4x8 slice. The times are simulated.
256 devices in a mesh: seq: 64 (over x_hi, z, y), mp: 4 (over x_lo, core).
Axes of the slice: x: 4 (x_hi: 2, x_lo: 2; x = x_hi * 2 + x_lo), y: 4, z: 8, core: 2. Of those that a mesh axis runs over, the one named last changes fastest.
Arguments:
- gate_in: bfloat16 [65536, 1024], P('seq', 'mp'), may hold values from -5 to 5
- value_in: bfloat16 [65536, 1024], P('seq', 'mp'), may hold values from -5 to 5
- out_gate: bfloat16 [65536, 1024], P('seq', 'mp'), may hold values from -10 to 10
- filter_taps: bfloat16 [4096, 1024], P('seq', 'mp'), may hold values from -0.09375 to 0.09375
- skip_gain: float32 [1024], P('mp'), may hold values from -4 to 4
Outputs:
- output: bfloat16 [65536, 1024], P('seq', 'mp')
All inputs are finite; a program needn't handle non-finite values.
Results may differ from a plain program's by a relative error of at most 0.009.
Values may be sent and summed in bfloat16 or wider, within the bound.
No kernel may reach another device: no remote copies, remote signals or barrier semaphores. Data moves between devices by JAX's collectives and lax.ppermute only.
A program may use at most 64 MiB of HBM per device.

v0:
```python
import math

import jax
import jax.numpy as jnp
from jax import lax
from jax.sharding import PartitionSpec as P

C = 1024
K = 4096
P_SIZE = 128


def shortened(shard):
    return jax.tree.map(lambda a: a.astype(jnp.bfloat16) if a.dtype == jnp.float32 else a, shard)


def from_everyone(shard, axis):
    copies = jnp.broadcast_to(shard, (lax.axis_size(axis), *shard.shape))
    return lax.all_to_all(copies, axis, split_axis=0, concat_axis=0, tiled=True)


def over_copies(shard, axis):
    everything = from_everyone(shard, axis)
    return jnp.sum(everything, axis=0)


def dft_tables(block):
    frame_len = 2 * block
    sample = lax.iota(jnp.int32, frame_len)[:, None]
    frequency = lax.iota(jnp.int32, block)[None, :]
    angles = (sample * frequency % frame_len).astype(jnp.float32) * (2.0 * math.pi / frame_len)
    alternate = jnp.where(sample % 2 == 0, 1.0, -1.0).astype(jnp.float32)
    forward = jnp.concatenate(
        [jnp.cos(angles), jnp.where(frequency == 0, alternate, -jnp.sin(angles))], axis=1
    )
    later = block + lax.iota(jnp.int32, block)[None, :]
    column = lax.iota(jnp.int32, block)[:, None]
    back_angles = (column * later % frame_len).astype(jnp.float32) * (2.0 * math.pi / frame_len)
    back_sign = jnp.where(later % 2 == 0, 1.0, -1.0).astype(jnp.float32)
    inv_real = jnp.where(column == 0, 1.0, 2.0 * jnp.cos(back_angles)) / frame_len
    inv_imag = jnp.where(column == 0, back_sign, -2.0 * jnp.sin(back_angles)) / frame_len
    backward = jnp.concatenate([inv_real, inv_imag], axis=0)
    return (forward, backward)


def split_table(table):
    upper_part = table.astype(jnp.bfloat16)
    lower_part = (table - upper_part.astype(jnp.float32)).astype(jnp.bfloat16)
    return (upper_part, lower_part)


def transform_rows(form, data, table):
    upper_part, lower_part = split_table(table)
    first = jnp.einsum(form, data, upper_part, preferred_element_type=jnp.float32)
    return first + jnp.einsum(form, data, lower_part, preferred_element_type=jnp.float32)


def filter_spectra(portion):
    forward, backward = dft_tables(P_SIZE)
    channels = portion.shape[1]
    segments = portion.reshape(-1, P_SIZE, channels)
    return transform_rows("snc,nf->scf", segments, forward[:P_SIZE])


def convolve(window, filter_spec):
    forward, backward = dft_tables(P_SIZE)
    channels = window.shape[1]
    blocks = window.reshape(-1, P_SIZE, channels)
    frames = jnp.concatenate([blocks[:-1], blocks[1:]], axis=1)
    spectra = transform_rows("mnc,nf->mcf", frames, forward)
    frame_count = spectra.shape[0]
    seg_count = filter_spec.shape[0]
    features = channels * 2 * P_SIZE
    lhs_data = spectra.reshape(1, frame_count, features)
    spec_real = filter_spec[..., :P_SIZE]
    spec_imag = filter_spec[..., P_SIZE:]
    kernel_real = jnp.concatenate([spec_real, spec_real], axis=-1)
    kernel_imag = jnp.concatenate([spec_imag, spec_imag], axis=-1)
    kernel = jnp.stack([kernel_real, kernel_imag], axis=-1)[::-1].reshape(
        seg_count, 1, features * 2
    )
    merged = lax.conv_general_dilated(
        lhs_data,
        kernel,
        (1,),
        "VALID",
        dimension_numbers=("NWC", "WIO", "NWC"),
        feature_group_count=features,
        precision=lax.Precision.HIGH,
    )
    merged = merged.reshape(-1, channels, 2 * P_SIZE, 2)
    with_real = merged[..., 0]
    with_imag = merged[..., 1]
    first_col = lax.iota(jnp.int32, P_SIZE) == 0
    out_real = with_real[..., :P_SIZE] - jnp.where(first_col, 0.0, with_imag[..., P_SIZE:])
    out_imag = jnp.where(
        first_col, with_imag[..., P_SIZE:], with_imag[..., :P_SIZE] + with_real[..., P_SIZE:]
    )
    joined = jnp.concatenate([out_real, out_imag], axis=-1)
    result = jnp.einsum("bcf,fn->bnc", joined, backward, precision=lax.Precision.HIGH)
    return result.reshape(-1, channels)


def local(gate_in, value_in, out_gate, filter_taps, skip_gain):
    gated = (gate_in.astype(jnp.float32) * value_in.astype(jnp.float32)).astype(jnp.bfloat16)
    by_channel, taps_channel = (
        lax.all_to_all(gated, "seq", split_axis=1, concat_axis=0, tiled=True),
        lax.all_to_all(filter_taps, "seq", split_axis=1, concat_axis=0, tiled=True),
    )
    leading = jnp.zeros((K, by_channel.shape[1]), jnp.bfloat16)
    window = jnp.concatenate([leading, by_channel], axis=0)
    filter_spec = filter_spectra(taps_channel)
    channel_result = convolve(window, filter_spec)
    convolved = lax.all_to_all(
        shortened(channel_result), "seq", split_axis=0, concat_axis=1, tiled=True
    ).astype(channel_result.dtype)
    gated_out = out_gate.astype(jnp.float32) * (
        convolved + skip_gain[None, :] * gated.astype(jnp.float32)
    )
    squares = jnp.sum(gated_out * gated_out, axis=1)
    totals = over_copies(squares, "mp")
    return (gated_out / jnp.sqrt(totals[:, None] / C + 1e-05)).astype(jnp.bfloat16)


def solution(mesh):
    return jax.shard_map(
        local,
        mesh=mesh,
        in_specs=(P("seq", "mp"), P("seq", "mp"), P("seq", "mp"), P("seq", "mp"), P("mp")),
        out_specs=P("seq", "mp"),
        check_vma=False,
    )
```

profile of v0, /device:TPU:1, one launch (start us, length us, event | category | flops | bytes accessed | tf_op | source)
XLA Modules:
  0.0 138.5 jit_solution(6606847997319983063)
XLA Ops:
  0.0 0.9 copy.56
  0.9 0.7 reshape.118
  1.6 15.1 %all-to-all-start.1 = ((bf16[64,2,128]{2,1,0:T(2,128)(2,1)}), bf16[64,2,128]{2,1,0:T(2,128)(2,1)S(1)}, u32[]{:S(2)}, u32[]{:S(2)}) async-start(bf16[64,2,128]{2,1,0:T(2,128)(2,1)} %reshape.118), calls=%async_computation.1 | async-start | bytes 65536 | tf_op jit(solution)/shard_map/all_to_all | solution.py:108
  16.7 1.2 copy.53
  18.0 1.2 copy.54
  19.2 0.5 negate_select_fusion.2
  19.8 0.2 multiply_convert_fusion
  20.0 0.4 select_multiply_fusion.1
  20.3 1.0 all_to_all.38
  21.3 6.3 %all-to-all-done.1 = bf16[64,2,128]{2,1,0:T(2,128)(2,1)S(1)} async-done(((bf16[64,2,128]{2,1,0:T(2,128)(2,1)}), bf16[64,2,128]{2,1,0:T(2,128)(2,1)S(1)}, u32[]{:S(2)}, u32[]{:S(2)}) %all-to-all-start.1) | async-done | bytes 32800 | tf_op jit(solution)/shard_map/all_to_all | solution.py:108
  27.6 6.1 %all-to-all-start = ((bf16[1024,64,4]{0,2,1:T(4,128)(2,1)}), bf16[1024,64,4]{0,2,1:T(4,128)(2,1)S(1)}, u32[]{:S(2)}, u32[]{:S(2)}) async-start(bf16[1024,64,4]{0,2,1:T(4,128)(2,1)} %all_to_all.38), calls=%async_computation | async-start | bytes 1048576 | tf_op jit(solution)/shard_map/all_to_all | solution.py:107
  33.8 0.1 reshape.119
  33.9 0.1 reshape.106
  34.0 0.2 fusion.32
  34.2 0.2 fusion.10
  34.4 0.1 rev.3
  34.5 0.2 copy.67
  34.7 0.3 reshape.116
  35.0 15.3 %all-to-all-done = bf16[1024,64,4]{0,2,1:T(4,128)(2,1)S(1)} async-done(((bf16[1024,64,4]{0,2,1:T(4,128)(2,1)}), bf16[1024,64,4]{0,2,1:T(4,128)(2,1)S(1)}, u32[]{:S(2)}, u32[]{:S(2)}) %all-to-all-start) | async-done | bytes 524320 | tf_op jit(solution)/shard_map/all_to_all | solution.py:107
  50.3 0.3 pad_slice_fusion
  50.7 0.8 slice.41
  51.5 0.1 constant_dynamic-update-slice_fusion.1
  51.6 0.8 slice.43
  52.4 0.1 constant_dynamic-update-slice_fusion
  52.6 0.5 fusion.14
  53.0 0.4 convolution_add_fusion
  53.5 1.4 %copy.55 = f32[543,4,256]{2,1,0:T(4,128)S(1)} copy(f32[543,4,256]{2,0,1:T(8,128)S(1)} %convolution_add_fusion) | data formatting | bytes 4448256 | tf_op jit(solution)/shard_map/add | solution.py:55
  54.9 4.0 %reshape.115 = f32[1,543,1024,1]{2,0,3,1:T(1,128)} reshape(f32[543,4,256]{2,1,0:T(4,128)S(1)} %copy.55) | data formatting | bytes 4448256 | tf_op jit(solution)/shard_map/reshape.1
  59.0 30.5 %convolution_reduce_fusion = f32[512,1024,2]{1,2,0:T(2,128)} fusion(f32[1,543,1024,1]{2,0,3,1:T(1,128)} %reshape.115, f32[32,1,1024,2]{2,1,3,0:T(1,128)S(1)} %reshape.116), kind=kOutput, calls=%fused_computation.19 | convolution fusion | flops 201326592 | bytes 6680576 | tf_op jit(solution)/shard_map/convolution
  89.5 7.0 %reshape.108 = f32[512,4,256,2]{2,1,3,0:T(4,128)} reshape(f32[512,1024,2]{1,2,0:T(2,128)} %convolution_reduce_fusion) | data formatting | bytes 8388608 | tf_op jit(solution)/shard_map/reshape | solution.py:91
  96.4 2.9 %fusion.48 = (f32[512,4,256,1]{2,1,3,0:T(4,128)S(1)}, f32[512,4,256,1]{2,1,3,0:T(4,128)S(1)}) fusion(f32[512,4,256,2]{2,1,3,0:T(4,128)} %reshape.108), kind=kLoop, calls=%fused_computation.82 | loop fusion | bytes 8388608 | tf_op jit(solution)/shard_map/slice | solution.py:93
  99.4 0.4 copy.74
  99.8 0.4 copy.75
  100.2 0.2 slice_subtract_fusion
  100.4 1.2 fusion.7
  101.6 0.0 copy-start
  101.7 0.3 copy.63
  101.9 0.2 convert_element_type.80
  102.2 1.2 copy.64
  103.4 7.3 %all-to-all-start.2 = ((bf16[64,1024,4]{1,2,0:T(4,128)(2,1)}), bf16[64,1024,4]{1,2,0:T(4,128)(2,1)S(1)}, u32[]{:S(2)}, u32[]{:S(2)}) async-start(bf16[64,1024,4]{1,2,0:T(4,128)(2,1)} %copy.64), calls=%async_computation.2 | async-start | bytes 1048576 | tf_op jit(solution)/shard_map/all_to_all | solution.py:114
  110.6 0.0 copy-done
  110.7 0.2 copy.52
  110.9 0.0 copy-start.1
  110.9 16.0 %all-to-all-done.2 = bf16[64,1024,4]{1,2,0:T(4,128)(2,1)S(1)} async-done(((bf16[64,1024,4]{1,2,0:T(4,128)(2,1)}), bf16[64,1024,4]{1,2,0:T(4,128)(2,1)S(1)}, u32[]{:S(2)}, u32[]{:S(2)}) %all-to-all-start.2) | async-done | bytes 524320 | tf_op jit(solution)/shard_map/all_to_all | solution.py:114
  126.9 0.1 convert_bitcast_fusion
  127.0 0.4 reshape.109
  127.4 0.0 copy-done.1
  127.4 0.3 multiply_reduce_fusion
  127.7 9.5 %all_to_all.51 = f32[4,1,1024]{2,1,0:T(1,128)S(1)} all-to-all(f32[4,1,1024]{2,1,0:T(1,128)S(1)} %broadcast_in_dim.103), channel_id=1, replica_groups=mesh['seq'=64,'mp'=4] {'mp'}, dimensions={0} | all-to-all | bytes 32768 | tf_op jit(solution)/shard_map/all_to_all | solution.py:19
  137.2 0.3 divide_convert_fusion
  137.5 1.0 copy.66
  (13 shorter events, 0.1 us)
Async XLA Ops:
  1.6 26.0 %all-to-all-start.1 = ((bf16[64,2,128]{2,1,0:T(2,128)(2,1)}), bf16[64,2,128]{2,1,0:T(2,128)(2,1)S(1)}, u32[]{:S(2)}, u32[]{:S(2)}) async-start(bf16[64,2,128]{2,1,0:T(2,128)(2,1)} %reshape.118), calls=%async_computation.1 | async-start | bytes 65536 | tf_op jit(solution)/shard_map/all_to_all | solution.py:108
  27.6 22.7 %all-to-all-start = ((bf16[1024,64,4]{0,2,1:T(4,128)(2,1)}), bf16[1024,64,4]{0,2,1:T(4,128)(2,1)S(1)}, u32[]{:S(2)}, u32[]{:S(2)}) async-start(bf16[1024,64,4]{0,2,1:T(4,128)(2,1)} %all_to_all.38), calls=%async_computation | async-start | bytes 1048576 | tf_op jit(solution)/shard_map/all_to_all | solution.py:107
  101.6 9.0 %copy-start = (bf16[1024,256]{1,0:T(8,128)(2,1)S(1)}, bf16[1024,256]{1,0:T(8,128)(2,1)}, u32[]{:S(2)}) copy-start(bf16[1024,256]{1,0:T(8,128)(2,1)} %param.7) | copy-start | bytes 1572868
  103.4 23.5 %all-to-all-start.2 = ((bf16[64,1024,4]{1,2,0:T(4,128)(2,1)}), bf16[64,1024,4]{1,2,0:T(4,128)(2,1)S(1)}, u32[]{:S(2)}, u32[]{:S(2)}) async-start(bf16[64,1024,4]{1,2,0:T(4,128)(2,1)} %copy.64), calls=%async_computation.2 | async-start | bytes 1048576 | tf_op jit(solution)/shard_map/all_to_all | solution.py:114
  110.9 16.5 %copy-start.1 = (f32[256]{0:T(256)S(1)}, f32[256]{0:T(256)}, u32[]{:S(2)}) copy-start(f32[256]{0:T(256)} %param.9) | copy-start | bytes 3076
where the time goes:
time: 140 us; the launch traced here: 139 us
  waiting for transfers between devices  37.6 us (27%)
  matrix products  32.9 us (24%)
  starting transfers between devices  28.5 us (20%)
  local copies, waits for them, and re-layouts  27.6 us (20%)
  blocking collectives  9.49 us (7%)
  other arithmetic  2.11 us (2%)
    another operation x1, matrix products  30.5 us
    all_to_all x1, waiting for transfers between devices, local(): lax.all_to_all(shortened(channel_result), 'seq', split_axis=0, concat_axi...  16 us
    all_to_all x1, waiting for transfers between devices, local(): lax.all_to_all(gated, 'seq', split_axis=1, concat_axis=0, tiled=True)  15.3 us
    all_to_all x1, starting transfers between devices, local(): lax.all_to_all(filter_taps, 'seq', split_axis=1, concat_axis=0, tiled=True)  15.1 us
    all_to_all x1, blocking collectives, from_everyone(): return lax.all_to_all(copies, axis, split_axis=0, concat_axis=0, tiled=True)  9.49 us
    all_to_all x1, starting transfers between devices, local(): lax.all_to_all(shortened(channel_result), 'seq', split_axis=0, concat_axi...  7.28 us
    reshape x1, local copies, waits for them, and re-layouts, convolve(): merged = merged.reshape(-1, channels, 2 * P_SIZE, 2)  6.99 us
    all_to_all x1, waiting for transfers between devices, local(): lax.all_to_all(filter_taps, 'seq', split_axis=1, concat_axis=0, tiled=True)  6.29 us
  transfers between devices with their start and end apart: 3, of which 3 were waited for; matrix products, arithmetic and copies ran while one was open for 4% of the time, Pallas kernels for 0%

commit v1 on v0

v1 whole, which is shorter than its diff:
```python
import functools
import jax
import jax.numpy as jnp
from jax import lax
from jax.experimental import pallas as pl
from jax.experimental.pallas import tpu as pltpu
from jax.sharding import PartitionSpec as P

CH = 1024
TAPS = 4096
BLOCK = 256
LAGS = TAPS // BLOCK
NT = (((1,), (1,)), ((), ()))
F32 = jnp.float32
BF16 = jnp.bfloat16


def identity(n):
    row = lax.broadcasted_iota(jnp.int32, (n, n), 0)
    col = lax.broadcasted_iota(jnp.int32, (n, n), 1)
    return jnp.where(row == col, 1.0, 0.0).astype(BF16)


def flipped(eye, block):
    return lax.dot_general(eye, block, NT, preferred_element_type=F32)


def gate_kernel(gate_ref, value_ref, taps_ref, out_ref, taps_out_ref, rows_ref):
    tokens, channels = gate_ref.shape
    peers = out_ref.shape[0]
    per_peer = channels // peers
    eye = identity(channels)
    for b in range(tokens // 128):
        part = pl.ds(b * 128, 128)
        gated = (gate_ref[part, :].astype(F32) * value_ref[part, :].astype(F32)).astype(BF16)
        rows_ref[b, :channels, :] = flipped(eye, gated)
    count = tokens // 128
    flat = rows_ref.reshape(count * rows_ref.shape[1], 128)
    pitch = rows_ref.shape[1]
    for j in range(peers):
        got = [flat[pl.ds(q * peers + j, count, stride=pitch), :] for q in range(per_peer)]
        out_ref[j] = jnp.concatenate(got, axis=0).astype(BF16)
    taps_out_ref[...] = flipped(eye, taps_ref[...]).astype(BF16)


def conv_kernel(where_ref, skip_ref, x_ref, taps_ref, out_ref, flat_ref, even_ref, odd_ref, wide_ref, out_rows):
    per_peer = taps_ref.shape[0]
    sources = 64
    segs = 8
    per_seg = sources // segs
    positions = per_seg * 4
    rows = positions * segs
    chunk = per_peer * 8
    pitch = per_seg * chunk + 8
    for g in range(segs):
        flat_ref[pl.ds(g * pitch, per_seg * chunk), :] = x_ref[pl.ds(g * per_seg * chunk, per_seg * chunk), :].astype(F32)
    lane = lax.broadcasted_iota(jnp.int32, (16, 128), 1)
    sub = lax.broadcasted_iota(jnp.int32, (16, 128), 0)
    first = lax.broadcasted_iota(jnp.int32, (8, 128), 0) == 0

    wide_ref[:, :128] = jnp.zeros((128, 128), BF16)
    wide_ref[:, 34 * 128:] = jnp.zeros((128, 128), BF16)

    def channel(q, _):
        before = [jnp.zeros((16, 128), BF16)] * 8
        for j in range(33):
            if j < 32:
                line = jnp.broadcast_to(taps_ref[q, pl.ds(j, 1), :], (16, 128))
                base = pltpu.roll(line, 0, 1, stride=1, stride_axis=0)
                now = [pltpu.roll(base, 16 * i, 1).astype(BF16) if i else base.astype(BF16) for i in range(8)]
            else:
                now = [jnp.zeros((16, 128), BF16)] * 8
            for i in range(8):
                wide_ref[pl.ds(16 * i, 16), pl.ds(128 * (j + 1), 128)] = jnp.where(
                    lane >= sub + 16 * i, now[i], before[i]
                )
            before = now
        tiles = []
        for p in range(positions):
            halves = []
            for h in range(2):
                b = (p % 4) * 2 + h
                start = (p // 4) * chunk + q * 8 + b
                halves.append(flat_ref[pl.ds(start, 8, stride=pitch), :])
            tiles.append(jnp.concatenate(halves, axis=1))
        first2 = jnp.concatenate([first, first], axis=1)
        line = [jnp.where(first2, 0.0, pltpu.roll(tiles[p + positions - LAGS], 1, 0)) for p in range(LAGS)] + tiles
        for a in range(len(line) // 2):
            even_ref[pl.ds(16 * a, 16), :] = jnp.concatenate([line[2 * a], line[2 * a + 1]], axis=0).astype(BF16)
        for a in range(len(line) // 2 - 1):
            odd_ref[pl.ds(16 * a, 16), :] = jnp.concatenate([line[2 * a + 1], line[2 * a + 2]], axis=0).astype(BF16)
        acc = None
        for s in range(LAGS + 1):
            start = LAGS - s
            if start % 2 == 0:
                lhs = even_ref[pl.ds(start * 8, rows), :]
            else:
                lhs = odd_ref[pl.ds((start - 1) * 8, rows), :]
            u = s * BLOCK
            rhs = jnp.concatenate([wide_ref[:, u + 128:u + 384], wide_ref[:, u:u + 256]], axis=0)
            term = jnp.dot(lhs, rhs, preferred_element_type=F32)
            acc = term if acc is None else acc + term
        skip = skip_ref[q * sources + where_ref[0]]
        for p in range(positions):
            full = acc[8 * p:8 * p + 8] + skip * tiles[p]
            for h in range(2):
                out_rows[pl.ds((p * 2 + h) * 8, 8), :] = full[:, h * 128:(h + 1) * 128]
        for g in range(segs):
            for jj in range(per_seg):
                got = out_rows[pl.ds(jj * 64 + g, 8, stride=8), :]
                out_ref[g * per_seg + jj, pl.ds(pl.multiple_of(q * 8, 8), 8), :] = got.astype(BF16)
        return 0

    lax.fori_loop(0, per_peer, channel, 0)


def mix_kernel(conv_ref, og_ref, mixed_ref, square_ref, rows_ref):
    tokens, channels = og_ref.shape
    peers = conv_ref.shape[0]
    per_peer = channels // peers
    count = tokens // 128
    chunk = per_peer * count
    rows_ref[...] = conv_ref[...].reshape(peers * chunk, 128).astype(F32)
    eye = identity(channels)
    for b in range(count):
        gate = flipped(eye, og_ref[pl.ds(b * 128, 128), :])
        total = jnp.zeros((8, 128), F32)
        for q in range(per_peer):
            got = rows_ref[pl.ds(q * count + b, peers, stride=chunk), :]
            mixed = gate[q * peers:(q + 1) * peers] * got
            mixed_ref[b, pl.ds(q * peers, peers), :] = mixed
            total = total + jnp.sum((mixed * mixed).reshape(peers // 8, 8, 128), axis=0)
        square_ref[pl.ds(b, 1), :] = jnp.sum(total, axis=0, keepdims=True)


def norm_kernel(mixed_ref, square_ref, out_ref):
    count, channels, _ = mixed_ref.shape
    power = (square_ref[0] + square_ref[1] + square_ref[2] + square_ref[3]) * (1.0 / CH)
    scale = 1.0 / jnp.sqrt(power + 1e-05)
    eye = identity(128)
    for b in range(count):
        scaled = (mixed_ref[b] * scale[b:b + 1, :]).astype(BF16)
        out_ref[pl.ds(b * 128, 128), :] = flipped(eye, scaled).astype(BF16)


def shape(dims, dtype):
    return jax.ShapeDtypeStruct(dims, dtype)


VMEM = pl.BlockSpec(memory_space=pltpu.VMEM)
SMEM = pl.BlockSpec(memory_space=pltpu.SMEM)


def local(gate_in, value_in, out_gate, filter_taps, skip_gain):
    tokens, channels = gate_in.shape
    peers = lax.axis_size("seq")
    per_peer = channels // peers
    count = tokens // 128
    taps_here = filter_taps.shape[0]
    message, taps = pl.pallas_call(
        gate_kernel,
        out_shape=(shape((peers, per_peer * count, 128), BF16), shape((channels, taps_here), BF16)),
        in_specs=[VMEM] * 3,
        out_specs=(VMEM, VMEM),
        scratch_shapes=[pltpu.VMEM((count, channels + 8, 128), F32)],
        name="gate",
    )(gate_in, value_in, filter_taps)
    tap_rows = taps.reshape(per_peer, peers, taps_here).transpose(1, 0, 2).reshape(peers, 1, 2, 128)
    message = jnp.concatenate([message.reshape(peers, 16, 2, 128), tap_rows], axis=1)
    message = lax.all_to_all(message, "seq", split_axis=0, concat_axis=0, tiled=True)
    signal = message[:, :16].reshape(peers * per_peer * count, 128)
    taps = message[:, 16].reshape(peers, per_peer, taps_here).transpose(1, 0, 2).reshape(per_peer, 32, 128).astype(F32)
    where = lax.axis_index("seq").reshape(1).astype(jnp.int32)
    convolved = pl.pallas_call(
        conv_kernel,
        out_shape=shape((peers, per_peer * count, 128), BF16),
        in_specs=[SMEM, SMEM, VMEM, VMEM],
        out_specs=VMEM,
        scratch_shapes=[
            pltpu.VMEM((8 * (8 * per_peer * count + 8), 128), F32),
            pltpu.VMEM((384, 256), BF16),
            pltpu.VMEM((384, 256), BF16),
            pltpu.VMEM((128, 35 * 128), BF16),
            pltpu.VMEM((512, 128), F32),
        ],
        name="conv",
    )(where, skip_gain, signal, taps)
    convolved = lax.all_to_all(convolved, "seq", split_axis=0, concat_axis=0, tiled=True)
    mixed, squares = pl.pallas_call(
        mix_kernel,
        out_shape=(shape((count, channels, 128), F32), shape((count, 128), F32)),
        in_specs=[VMEM] * 2,
        out_specs=(VMEM, VMEM),
        scratch_shapes=[pltpu.VMEM((peers * per_peer * count, 128), F32)],
        name="mix",
    )(convolved, out_gate)
    squares = lax.all_gather(squares, "mp")
    return pl.pallas_call(
        norm_kernel,
        out_shape=shape((tokens, channels), BF16),
        in_specs=[VMEM] * 2,
        out_specs=VMEM,
        name="norm",
    )(mixed, squares)


def solution(mesh):
    return jax.shard_map(
        local,
        mesh=mesh,
        in_specs=(P("seq", "mp"), P("seq", "mp"), P("seq", "mp"), P("seq", "mp"), P("mp")),
        out_specs=P("seq", "mp"),
        check_vma=False,
    )
```

time: 140 us -> 87.1 us (0.62)
  matrix products: 32.9 us -> 0 us
  local copies, waits for them, and re-layouts: 27.6 us -> 3 us
  blocking collectives: 9.49 us -> 33 us
  waiting for transfers between devices: 37.6 us -> 18.2 us
  Pallas kernels: 0 us -> 14.7 us
  starting transfers between devices: 28.5 us -> 15.1 us
    another operation x1 -> x0, matrix products: 30.5 us -> none
    all_to_all x3 -> x1, waiting for transfers between devices: 37.6 us -> 18.2 us  [local(): lax.all_to_all(message, 'seq', split_axis=0, concat_axis=0, tiled=True)]
    pallas_call x0 -> x4, Pallas kernels: none -> 14.7 us  [the longest x1 6.7 us: local(): pl.pallas_call(conv_kernel, out_shape=shape((peers, per_peer * count, 128...]
    all_to_all x1, blocking collectives: 9.49 us -> 23.6 us  [local(): lax.all_to_all(convolved, 'seq', split_axis=0, concat_axis=0, tiled=True)]
    all_to_all x3 -> x1, starting transfers between devices: 28.5 us -> 15.1 us  [local(): lax.all_to_all(message, 'seq', split_axis=0, concat_axis=0, tiled=True)]
    all_gather x0 -> x1, blocking collectives: none -> 9.41 us  [local(): squares = lax.all_gather(squares, 'mp')]
    reshape x4 -> x1, local copies, waits for them, and re-layouts: 7.58 us -> 0.1 us  [local(): taps.reshape(per_peer, peers, taps_here).transpose(1, 0, 2)]
    unnamed x13 -> x0, local copies, waits for them, and re-layouts: 5.29 us -> none
  transfers between devices with their start and end apart: 3 -> 1, of which waited for: 3 -> 1; matrix products, arithmetic and copies ran while one was open for 4% -> 0% of each run, Pallas kernels for 0% -> 0%
where the time goes in v1:
time: 87.1 us; the launch traced here: 86.6 us
  blocking collectives  33 us (38%)
  waiting for transfers between devices  18.2 us (21%)
  starting transfers between devices  15.1 us (17%)
  Pallas kernels  14.7 us (17%)
  local copies, waits for them, and re-layouts  3 us (3%)
  other arithmetic  2.6 us (3%)
    all_to_all x1, blocking collectives, local(): lax.all_to_all(convolved, 'seq', split_axis=0, concat_axis=0, tiled=True)  23.6 us
    all_to_all x1, waiting for transfers between devices, local(): lax.all_to_all(message, 'seq', split_axis=0, concat_axis=0, tiled=True)  18.2 us
    all_to_all x1, starting transfers between devices, local(): lax.all_to_all(message, 'seq', split_axis=0, concat_axis=0, tiled=True)  15.1 us
    all_gather x1, blocking collectives, local(): squares = lax.all_gather(squares, 'mp')  9.41 us
    pallas_call x1, Pallas kernels, local(): pl.pallas_call(conv_kernel, out_shape=shape((peers, per_peer * count, 128...  6.7 us
    pallas_call x1, Pallas kernels, local(): pl.pallas_call(mix_kernel, out_shape=(shape((count, channels, 128), F32),...  2.98 us
    pallas_call x1, Pallas kernels, local(): pl.pallas_call(gate_kernel, out_shape=(shape((peers, per_peer * count, 12...  2.63 us
    concatenate x1, other arithmetic, local(): jnp.concatenate([message.reshape(peers, 16, 2, 128), tap_rows], axis=1)  2.57 us
  transfers between devices with their start and end apart: 1, of which 1 were waited for; matrix products, arithmetic and copies ran while one was open for 0% of the time, Pallas kernels for 0%

profile of v1, /device:TPU:1, one launch (start us, length us, event | category | flops | bytes accessed | tf_op | source)
XLA Modules:
  0.0 86.6 jit_solution(11574452574080209796)
XLA Ops:
  0.0 2.6 %gate.1 = (bf16[64,32,128]{2,1,0:T(8,128)(2,1)}, bf16[256,64]{1,0:T(8,128)(2,1)}) custom-call(bf16[1024,256]{1,0:T(8,128)(2,1)} %gate_ref.1, bf16[1024,256]{1,0:T(8,128)(2,1)} %value_ref.1, bf16[64,256]{1,0:T(8,128)(2,1)} %taps_ref.1), custom_call_target="tpu_custom_call" | custom-call | tf_op jit(solution)/shard_map/gate/pallas_call | solution.py:160
  2.6 0.9 %copy.11 = bf16[64,4,64]{2,1,0:T(4,128)(2,1)S(1)} copy(bf16[64,4,64]{2,0,1:T(8,128)(2,1)} %bitcast.12) | data formatting | bytes 65536 | tf_op jit(solution)/shard_map/transpose | solution.py:168
  3.5 0.1 reshape.23
  3.6 2.6 %pad_maximum_fusion = bf16[64,17,2,128]{3,2,1,0:T(2,128)(2,1)} fusion(bf16[64,1,2,128]{3,2,1,0:T(2,128)(2,1)S(1)} %reshape.23, bf16[64,16,2,128]{3,2,1,0:T(2,128)(2,1)} %bitcast.9), kind=kLoop, calls=%fused_computation | loop fusion | flops 278528 | bytes 1114112 | tf_op jit(solution)/shard_map/concatenate | solution.py:169
  6.2 15.1 %all-to-all-start = ((bf16[64,17,2,128]{3,2,1,0:T(2,128)(2,1)}), bf16[64,17,2,128]{3,2,1,0:T(2,128)(2,1)S(1)}, u32[]{:S(2)}, u32[]{:S(2)}) async-start(bf16[64,17,2,128]{3,2,1,0:T(2,128)(2,1)} %pad_maximum_fusion), calls=%async_computation | async-start | bytes 1114112 | tf_op jit(solution)/shard_map/all_to_all | solution.py:170
  21.3 18.2 %all-to-all-done = bf16[64,17,2,128]{3,2,1,0:T(2,128)(2,1)S(1)} async-done(((bf16[64,17,2,128]{3,2,1,0:T(2,128)(2,1)}), bf16[64,17,2,128]{3,2,1,0:T(2,128)(2,1)S(1)}, u32[]{:S(2)}, u32[]{:S(2)}) %all-to-all-start) | async-done | bytes 557088 | tf_op jit(solution)/shard_map/all_to_all | solution.py:170
  39.6 0.1 reshape.26
  39.7 0.7 reshape.25.taps_ref
  40.4 1.2 %slice.8 = bf16[64,16,2,128]{3,2,1,0:T(2,128)(2,1)} slice(bf16[64,17,2,128]{3,2,1,0:T(2,128)(2,1)S(1)} %all-to-all-done), slice={[0:64], [0:16], [0:2], [0:128]} | slice | bytes 1048576 | tf_op jit(solution)/shard_map/slice | solution.py:171
  41.6 6.7 %conv.1 = bf16[64,32,128]{2,1,0:T(8,128)(2,1)} custom-call(s32[1]{0:T(128)} %bitcast.where_ref, f32[256]{0:T(256)} %skip_ref.1, bf16[2048,128]{1,0:T(8,128)(2,1)} %bitcast.8, f32[4,32,128]{2,1,0:T(8,128)} %reshape.25.taps_ref), custom_call_target="tpu_custom_call" | custom-call | tf_op jit(solution)/shard_map/conv/pallas_call | solution.py:174
  48.3 23.6 %all_to_all.10.conv_ref = bf16[64,32,128]{2,1,0:T(8,128)(2,1)} all-to-all(bf16[64,32,128]{2,1,0:T(8,128)(2,1)} %conv.1), channel_id=1, replica_groups=mesh['seq'=64,'mp'=4] {'seq'}, dimensions={0} | all-to-all | bytes 1048576 | tf_op jit(solution)/shard_map/all_to_all | solution.py:188
  71.9 3.0 %mix.1 = (f32[8,256,128]{2,1,0:T(8,128)}, f32[8,128]{1,0:T(8,128)}) custom-call(bf16[64,32,128]{2,1,0:T(8,128)(2,1)} %all_to_all.10.conv_ref, bf16[1024,256]{1,0:T(8,128)(2,1)} %og_ref.1), custom_call_target="tpu_custom_call" | custom-call | tf_op jit(solution)/shard_map/mix/pallas_call | solution.py:189
  74.8 9.4 %all-gather = f32[32,128]{1,0:T(8,128)} all-gather(f32[8,128]{1,0:T(8,128)} %get-tuple-element.12), channel_id=2, replica_groups=mesh['seq'=64,'mp'=4] {'mp'}, dimensions={0}, use_global_device_ids=true | all-gather | bytes 20480 | tf_op jit(solution)/shard_map/all_gather | solution.py:197
  84.2 2.4 %norm.1 = bf16[1024,256]{1,0:T(8,128)(2,1)} custom-call(f32[8,256,128]{2,1,0:T(8,128)} %get-tuple-element.11.mixed_ref, f32[4,8,128]{2,1,0:T(8,128)} %bitcast.11), custom_call_target="tpu_custom_call" | custom-call | tf_op jit(solution)/shard_map/norm/pallas_call | solution.py:198
  (2 shorter events, 0.0 us)
Async XLA Ops:
  6.2 33.3 %all-to-all-start = ((bf16[64,17,2,128]{3,2,1,0:T(2,128)(2,1)}), bf16[64,17,2,128]{3,2,1,0:T(2,128)(2,1)S(1)}, u32[]{:S(2)}, u32[]{:S(2)}) async-start(bf16[64,17,2,128]{3,2,1,0:T(2,128)(2,1)} %pad_maximum_fusion), calls=%async_computation | async-start | bytes 1114112 | tf_op jit(solution)/shard_map/all_to_all | solution.py:170

commit v2 on v1

v2 whole, which is shorter than its diff:
```python
import jax
import jax.numpy as jnp
from jax import lax
from jax.experimental import pallas as pl
from jax.experimental.pallas import tpu as pltpu
from jax.sharding import PartitionSpec as P

CH = 1024
TAPS = 4096
BLOCK = 256
LAGS = TAPS // BLOCK
SEGS = 8
NT = (((1,), (1,)), ((), ()))
F32 = jnp.float32
BF16 = jnp.bfloat16
MIB = 1024 * 1024


def identity(n):
    row = lax.broadcasted_iota(jnp.int32, (n, n), 0)
    col = lax.broadcasted_iota(jnp.int32, (n, n), 1)
    return jnp.where(row == col, 1.0, 0.0).astype(BF16)


def flipped(eye, block):
    return lax.dot_general(eye, block, NT, preferred_element_type=F32)


def gate_kernel(gated_ref, og_ref, taps_ref, skip_ref, out_ref, og_out_ref, skip_out_ref, rows_ref, og_rows_ref):
    skip_out_ref[...] = skip_ref[...]
    tokens, channels = gated_ref.shape
    count = tokens // 128
    pitch = og_rows_ref.shape[0] // count
    chunk = 34
    peers = out_ref.shape[0] // chunk
    per_peer = channels // peers
    eye = identity(channels)
    turned = flipped(eye, taps_ref[...])
    wide = (2 * count + 8) * pitch
    for r in range(2):
        rows_ref[pl.ds(wide + r * (peers + 8), peers), :] = jnp.concatenate(
            [turned[2 * r * peers:(2 * r + 1) * peers], turned[(2 * r + 1) * peers:(2 * r + 2) * peers]], axis=1
        )
    front = 8 * pitch
    for b in range(0, count, 2):
        turned = flipped(eye, gated_ref[pl.ds(b * 128, 256), :])
        for n in range(2):
            rows_ref[pl.ds(front + (b + n) * pitch, channels), :] = turned[:, n * 128:(n + 1) * 128]
        turned = flipped(eye, og_ref[pl.ds(b * 128, 256), :])
        for n in range(2):
            og_rows_ref[pl.ds((b + n) * pitch, channels), :] = turned[:, n * 128:(n + 1) * 128]
    sub = lax.broadcasted_iota(jnp.int32, (8, 128), 0)

    def tile(first):
        runs = []
        row = first
        while row < first + 8:
            j, r = divmod(row, chunk)
            at = row - first
            if r < 32:
                q, b = divmod(r, count)
                base = front + q * peers + j + (b - at) * pitch
                runs.append((at, rows_ref[pl.ds(base, 8, stride=pitch), :]))
                row += count - b
            else:
                base = wide + j + (r - 32 - at) * (peers + 8)
                runs.append((at, rows_ref[pl.ds(base, 8, stride=peers + 8), :]))
                row += 34 - r
        value = runs[0][1]
        for at, more in runs[1:]:
            value = jnp.where(sub >= at, more, value)
        return value

    for n in range(peers * chunk // 16):
        out_ref[pl.ds(n * 16, 16), :] = jnp.concatenate([tile(n * 16), tile(n * 16 + 8)], axis=0).astype(BF16)
    for j in range(peers):
        got = [og_rows_ref[pl.ds(q * peers + j, count, stride=pitch), :] for q in range(per_peer)]
        og_out_ref[pl.ds(j * 32, 32), :] = jnp.concatenate(got, axis=0).astype(BF16)


def conv_kernel(skip_ref, x_ref, out_ref, flat_ref, taps_ref, even_ref, odd_ref, wide_ref, out_rows):
    chunk = 34
    sources = x_ref.shape[0] // chunk
    per_peer = 4
    per_seg = sources // SEGS
    positions = per_seg * 4
    rows = positions * SEGS
    pitch = flat_ref.shape[0] // SEGS
    for g in range(SEGS):
        flat_ref[pl.ds(g * pitch, per_seg * chunk), :] = x_ref[pl.ds(g * per_seg * chunk, per_seg * chunk), :].astype(F32)
    low = lax.broadcasted_iota(jnp.int32, (4, 128), 1) < 64
    for r in range(2):
        for g in range(SEGS):
            even = flat_ref[pl.ds(g * pitch + 32 + r, 4, stride=2 * chunk), :]
            odd = flat_ref[pl.ds(g * pitch + chunk + 32 + r, 4, stride=2 * chunk), :]
            taps_ref[2 * r, pl.ds(4 * g, 4), :] = jnp.where(low, even, pltpu.roll(odd, 64, 1))
            taps_ref[2 * r + 1, pl.ds(4 * g, 4), :] = jnp.where(low, pltpu.roll(even, 64, 1), odd)
    lane = lax.broadcasted_iota(jnp.int32, (16, 128), 1)
    sub = lax.broadcasted_iota(jnp.int32, (16, 128), 0)
    first = lax.broadcasted_iota(jnp.int32, (8, 256), 0) == 0
    for q in range(per_peer):
        wide_ref[q, :, :128] = jnp.zeros((128, 128), BF16)
        wide_ref[q, :, 34 * 128:] = jnp.zeros((128, 128), BF16)

    for q in range(per_peer):
        before = [jnp.zeros((16, 128), BF16)] * 8
        for j in range(33):
            if j < 32:
                line = jnp.broadcast_to(taps_ref[q, pl.ds(j, 1), :], (16, 128))
                base = pltpu.roll(line, 0, 1, stride=1, stride_axis=0)
                now = [pltpu.roll(base, 16 * i, 1).astype(BF16) if i else base.astype(BF16) for i in range(8)]
            else:
                now = [jnp.zeros((16, 128), BF16)] * 8
            for i in range(8):
                wide_ref[q, pl.ds(16 * i, 16), pl.ds(128 * (j + 1), 128)] = jnp.where(
                    lane >= sub + 16 * i, now[i], before[i]
                )
            before = now
        tiles = []
        for p in range(positions):
            halves = []
            for h in range(2):
                start = (p // 4) * chunk + q * 8 + (p % 4) * 2 + h
                halves.append(flat_ref[pl.ds(start, 8, stride=pitch), :])
            tiles.append(jnp.concatenate(halves, axis=1))
        line = [jnp.where(first, 0.0, pltpu.roll(tiles[p + positions - LAGS], 1, 0)) for p in range(LAGS)] + tiles
        for a in range(len(line) // 2):
            even_ref[q, pl.ds(16 * a, 16), :] = jnp.concatenate([line[2 * a], line[2 * a + 1]], axis=0).astype(BF16)
        for a in range(len(line) // 2 - 1):
            odd_ref[q, pl.ds(16 * a, 16), :] = jnp.concatenate([line[2 * a + 1], line[2 * a + 2]], axis=0).astype(BF16)
        acc = None
        for s in range(LAGS + 1):
            start = LAGS - s
            if start % 2 == 0:
                lhs = even_ref[q, pl.ds(start * 8, rows), :]
            else:
                lhs = odd_ref[q, pl.ds((start - 1) * 8, rows), :]
            u = s * BLOCK
            rhs = jnp.concatenate([wide_ref[q, :, u + 128:u + 384], wide_ref[q, :, u:u + 256]], axis=0)
            term = jnp.dot(lhs, rhs, preferred_element_type=F32)
            acc = term if acc is None else acc + term
        mine = lax.broadcasted_iota(jnp.int32, (2, 128), 0) * 128 + lax.broadcasted_iota(jnp.int32, (2, 128), 1)
        mine = jnp.where(mine == q * sources + lax.axis_index("seq"), skip_ref[...], 0.0)
        skip = jnp.sum(jnp.sum(mine, axis=1, keepdims=True), axis=0, keepdims=True)
        for p in range(positions):
            for h in range(2):
                start = (p // 4) * chunk + q * 8 + (p % 4) * 2 + h
                own = flat_ref[pl.ds(start, 8, stride=pitch), :]
                out_rows[q, pl.ds((p * 2 + h) * 8, 8), :] = acc[8 * p:8 * p + 8, h * 128:(h + 1) * 128] + skip * own
    for j in range(sources):
        g, jj = divmod(j, per_seg)
        got = [out_rows[q, pl.ds(jj * 64 + g, 8, stride=8), :] for q in range(per_peer)]
        out_ref[pl.ds(j * 32, 32), :] = jnp.concatenate(got, axis=0).astype(BF16)


def square_kernel(conv_ref, og_ref, square_ref):
    def step(n, total):
        part = pl.ds(pl.multiple_of(n * 128, 128), 128)
        mixed = conv_ref[part, :].astype(F32) * og_ref[part, :].astype(F32)
        return total + (mixed * mixed).reshape(8, 16, 128)

    total = lax.fori_loop(0, conv_ref.shape[0] // 128, step, jnp.zeros((8, 16, 128), F32), unroll=True)
    total = jnp.sum(total, axis=0)
    square_ref[...] = total[:8] + total[8:]


def norm_kernel(conv_ref, og_ref, square_ref, out_hbm, rows_ref, out_ref, sems):
    rows = conv_ref.shape[0]
    tokens, channels = out_ref.shape
    count = tokens // 128
    peers = rows // 32
    per_peer = channels // peers
    power = (square_ref[0] + square_ref[1] + square_ref[2] + square_ref[3]) * (1.0 / CH)
    scale = 1.0 / jnp.sqrt(power + 1e-05)
    scale = jnp.concatenate([scale, scale], axis=0)
    for n in range(rows // 16):
        part = pl.ds(n * 16, 16)
        rows_ref[part, :] = conv_ref[part, :].astype(F32) * og_ref[part, :].astype(F32) * scale
    eye = identity(128)
    copies = []
    for b in range(count):
        got = [rows_ref[pl.ds(q * count + b, peers, stride=32), :] for q in range(per_peer)]
        part = pl.ds(b * 128, 128)
        out_ref[part, :] = flipped(eye, jnp.concatenate(got, axis=0).astype(BF16)).astype(BF16)
        copies.append(pltpu.make_async_copy(out_ref.at[part], out_hbm.at[part], sems.at[b]))
        copies[-1].start()
    for copy in copies:
        copy.wait()


def shape(dims, dtype):
    return jax.ShapeDtypeStruct(dims, dtype)


VMEM = pl.BlockSpec(memory_space=pltpu.VMEM)
SMEM = pl.BlockSpec(memory_space=pltpu.SMEM)
HBM = pl.BlockSpec(memory_space=pltpu.HBM)


def params(mib):
    return pltpu.CompilerParams(vmem_limit_bytes=mib * MIB)


def local(gate_in, value_in, out_gate, filter_taps, skip_gain):
    tokens, channels = gate_in.shape
    peers = lax.axis_size("seq")
    per_peer = channels // peers
    count = tokens // 128
    rows = peers * per_peer * count
    gated = (gate_in.astype(F32) * value_in.astype(F32)).astype(BF16)
    message, turned, skip = pl.pallas_call(
        gate_kernel,
        out_shape=(shape((peers * 34, 128), BF16), shape((rows, 128), BF16), shape((channels // 128, 128), F32)),
        in_specs=[VMEM] * 4,
        out_specs=(VMEM,) * 3,
        scratch_shapes=[
            pltpu.VMEM(((2 * count + 8) * (channels + 8) + 16 * (peers + 8), 128), F32),
            pltpu.VMEM((count * (channels + 8), 128), F32),
        ],
        compiler_params=params(12),
        name="gate",
    )(gated, out_gate, filter_taps, skip_gain.reshape(channels // 128, 128))
    message = lax.all_to_all(message.reshape(peers, 17, 2, 128), "seq", split_axis=0, concat_axis=0, tiled=True)
    convolved = pl.pallas_call(
        conv_kernel,
        out_shape=shape((rows, 128), BF16),
        in_specs=[VMEM, VMEM],
        out_specs=VMEM,
        scratch_shapes=[
            pltpu.VMEM((SEGS * 280, 128), F32),
            pltpu.VMEM((4, 32, 128), F32),
            pltpu.VMEM((4, 384, 256), BF16),
            pltpu.VMEM((4, 384, 256), BF16),
            pltpu.VMEM((4, 128, 35 * 128), BF16),
            pltpu.VMEM((4, 512, 128), F32),
        ],
        compiler_params=params(24),
        name="conv",
    )(skip, message.reshape(peers * 34, 128))
    convolved = lax.all_to_all(
        convolved.reshape(peers, 32, 128), "seq", split_axis=0, concat_axis=0, tiled=True
    ).reshape(rows, 128)
    squares = pl.pallas_call(
        square_kernel,
        out_shape=shape((count, 128), F32),
        in_specs=[VMEM] * 2,
        out_specs=VMEM,
        compiler_params=params(8),
        name="square",
    )(convolved, turned)
    squares = lax.all_gather(squares, "mp")
    return pl.pallas_call(
        norm_kernel,
        out_shape=shape((tokens, channels), BF16),
        in_specs=[VMEM] * 3,
        out_specs=HBM,
        scratch_shapes=[
            pltpu.VMEM((rows, 128), F32),
            pltpu.VMEM((tokens, channels), BF16),
            pltpu.SemaphoreType.DMA((count,)),
        ],
        compiler_params=params(12),
        name="norm",
    )(convolved, turned, squares)


def solution(mesh):
    return jax.shard_map(
        local,
        mesh=mesh,
        in_specs=(P("seq", "mp"), P("seq", "mp"), P("seq", "mp"), P("seq", "mp"), P("mp")),
        out_specs=P("seq", "mp"),
        check_vma=False,
    )
```

time: 87.1 us -> 75.2 us (0.86)
  blocking collectives: 33 us -> 65.2 us
  waiting for transfers between devices: 18.2 us -> 0 us
  starting transfers between devices: 15.1 us -> 0 us
  Pallas kernels: 14.7 us -> 7.72 us
  local copies, waits for them, and re-layouts: 3 us -> 0.66 us
  other arithmetic: 2.6 us -> 1.39 us
    all_to_all x1 -> x2, blocking collectives: 23.6 us -> 56.4 us  [the longest x1 33.1 us: local(): lax.all_to_all(message.reshape(peers, 17, 2, 128), 'seq', split_axis=0, c...]
    all_to_all x1 -> x0, waiting for transfers between devices: 18.2 us -> none  [local(): lax.all_to_all(message, 'seq', split_axis=0, concat_axis=0, tiled=True)]
    all_to_all x1 -> x0, starting transfers between devices: 15.1 us -> none  [local(): lax.all_to_all(message, 'seq', split_axis=0, concat_axis=0, tiled=True)]
    pallas_call x3, Pallas kernels: 12.3 us -> 6.09 us  [the longest x1 4.88 us: local(): pl.pallas_call(conv_kernel, out_shape=shape((rows, 128), BF16), in_specs=...]
    concatenate x1 -> x0, other arithmetic: 2.57 us -> none  [local(): jnp.concatenate([message.reshape(peers, 16, 2, 128), tap_rows], axis=1)]
    convert_element_type x1, other arithmetic: 0.02 us -> 1.39 us  [local(): gated = (gate_in.astype(F32) * value_in.astype(F32)).astype(BF16)]
    slice x1 -> x0, local copies, waits for them, and re-layouts: 1.15 us -> none  [local(): signal = message[:, :16].reshape(peers * per_peer * count, 128)]
    transpose x1 -> x0, local copies, waits for them, and re-layouts: 0.89 us -> none  [local(): taps.reshape(per_peer, peers, taps_here).transpose(1, 0, 2)]
  transfers between devices with their start and end apart: 1 -> 0, of which waited for: 1 -> 0; matrix products, arithmetic and copies ran while one was open for 0% -> 0% of each run, Pallas kernels for 0% -> 0%
where the time goes in v2:
time: 75.2 us; the launch traced here: 75 us
  blocking collectives  65.2 us (87%)
  Pallas kernels  7.72 us (10%)
  other arithmetic  1.39 us (2%)
    all_to_all x1, blocking collectives, local(): lax.all_to_all(message.reshape(peers, 17, 2, 128), 'seq', split_axis=0, c...  33.1 us
    all_to_all x1, blocking collectives, local(): lax.all_to_all(convolved.reshape(peers, 32, 128), 'seq', split_axis=0, co...  23.2 us
    all_gather x1, blocking collectives, local(): squares = lax.all_gather(squares, 'mp')  8.83 us
    pallas_call x1, Pallas kernels, local(): pl.pallas_call(conv_kernel, out_shape=shape((rows, 128), BF16), in_specs=...  4.88 us
    pallas_call x1, Pallas kernels, local(): pl.pallas_call(norm_kernel, out_shape=shape((tokens, channels), BF16), in...  1.63 us

profile of v2, /device:TPU:1, one launch (start us, length us, event | category | flops | bytes accessed | tf_op | source)
XLA Modules:
  0.0 75.0 jit_solution(4972592479682814121)
XLA Ops:
  0.0 0.0 copy-start.1
  0.0 0.0 copy-start
  0.0 1.4 %multiply_convert_fusion.gated_ref = bf16[1024,256]{1,0:T(8,128)(2,1)S(1)} fusion(bf16[1024,256]{1,0:T(8,128)(2,1)} %param.6, bf16[1024,256]{1,0:T(8,128)(2,1)} %param.5), kind=kLoop, calls=%fused_computation | loop fusion | flops 1048576 | bytes 1572864 | tf_op jit(solution)/shard_map/convert_element_type | solution.py:210
  1.4 0.0 copy-start.2
  1.4 0.0 copy-done.1
  1.4 0.0 copy-done
  1.4 0.7 copy-done.2
  2.1 1.0 %gate.1 = (bf16[2176,128]{1,0:T(8,128)(2,1)S(1)}, bf16[2048,128]{1,0:T(8,128)(2,1)S(1)}, f32[2,128]{1,0:T(2,128)S(1)}) custom-call(bf16[1024,256]{1,0:T(8,128)(2,1)S(1)} %multiply_convert_fusion.gated_ref, bf16[1024,256]{1,0:T(8,128)(2,1)S(1)} %copy-done, bf16[64,256]{1,0:T(8,128)(2,1)S(1)} %copy-done.1, f32[2,128]{1,0:T(2,128)S(1)} %bitcast.12), custom_call_target="tpu_custom_call" | custom-call | tf_op jit(solution)/shard_map/gate/pallas_call | solution.py:211
  3.1 33.1 %all_to_all.10 = bf16[64,17,2,128]{3,2,1,0:T(2,128)(2,1)S(1)} all-to-all(bf16[64,17,2,128]{3,2,1,0:T(2,128)(2,1)S(1)} %bitcast.10), channel_id=1, replica_groups=mesh['seq'=64,'mp'=4] {'seq'}, dimensions={0} | all-to-all | bytes 1114112 | tf_op jit(solution)/shard_map/all_to_all | solution.py:223
  36.2 4.9 %conv.1 = bf16[2048,128]{1,0:T(8,128)(2,1)S(1)} custom-call(f32[2,128]{1,0:T(2,128)S(1)} %get-tuple-element.8.skip_ref, bf16[2176,128]{1,0:T(8,128)(2,1)S(1)} %bitcast.8), custom_call_target="tpu_custom_call" | custom-call | tf_op jit(solution)/shard_map/conv/pallas_call | solution.py:224
  41.1 23.2 %all_to_all.11 = bf16[64,32,128]{2,1,0:T(8,128)(2,1)S(1)} all-to-all(bf16[64,32,128]{2,1,0:T(8,128)(2,1)S(1)} %bitcast.9), channel_id=1, replica_groups=mesh['seq'=64,'mp'=4] {'seq'}, dimensions={0} | all-to-all | bytes 1048576 | tf_op jit(solution)/shard_map/all_to_all | solution.py:240
  64.3 0.2 square.1
  64.5 8.8 %all-gather = f32[32,128]{1,0:T(8,128)S(1)} all-gather(f32[8,128]{1,0:T(8,128)S(1)} %square.1), channel_id=2, replica_groups=mesh['seq'=64,'mp'=4] {'mp'}, dimensions={0}, use_global_device_ids=true | all-gather | bytes 20480 | tf_op jit(solution)/shard_map/all_gather | solution.py:251
  73.4 1.6 %norm.1 = bf16[1024,256]{1,0:T(8,128)(2,1)} custom-call(bf16[2048,128]{1,0:T(8,128)(2,1)S(1)} %bitcast.7, bf16[2048,128]{1,0:T(8,128)(2,1)S(1)} %get-tuple-element.10.og_ref, f32[4,8,128]{2,1,0:T(8,128)S(1)} %bitcast.11), custom_call_target="tpu_custom_call" | custom-call | tf_op jit(solution)/shard_map/norm/pallas_call | solution.py:252
Async XLA Ops:
  0.0 1.4 %copy-start.1 = (bf16[64,256]{1,0:T(8,128)(2,1)S(1)}, bf16[64,256]{1,0:T(8,128)(2,1)}, u32[]{:S(2)}) copy-start(bf16[64,256]{1,0:T(8,128)(2,1)} %taps_ref.1) | copy-start | bytes 98308
  0.0 1.4 %copy-start = (bf16[1024,256]{1,0:T(8,128)(2,1)S(1)}, bf16[1024,256]{1,0:T(8,128)(2,1)}, u32[]{:S(2)}) copy-start(bf16[1024,256]{1,0:T(8,128)(2,1)} %og_ref.1) | copy-start | bytes 1572868
  1.4 0.7 copy-start.2

commit v3 on v2

--- a/solution.py
+++ b/solution.py
@@ -10,6 +10,7 @@
 BLOCK = 256
 LAGS = TAPS // BLOCK
 SEGS = 8
+ROLLED = 6
 NT = (((1,), (1,)), ((), ()))
 F32 = jnp.float32
 BF16 = jnp.bfloat16
@@ -78,7 +79,7 @@
         og_out_ref[pl.ds(j * 32, 32), :] = jnp.concatenate(got, axis=0).astype(BF16)
 
 
-def conv_kernel(skip_ref, x_ref, out_ref, flat_ref, taps_ref, even_ref, odd_ref, wide_ref, out_rows):
+def conv_kernel(skip_ref, x_ref, out_ref, flat_ref, taps_ref, even_ref, odd_ref, steep_ref, shift_ref, wide_ref, out_rows):
     chunk = 34
     sources = x_ref.shape[0] // chunk
     per_peer = 4
@@ -97,46 +98,68 @@
             taps_ref[2 * r + 1, pl.ds(4 * g, 4), :] = jnp.where(low, pltpu.roll(even, 64, 1), odd)
     lane = lax.broadcasted_iota(jnp.int32, (16, 128), 1)
     sub = lax.broadcasted_iota(jnp.int32, (16, 128), 0)
-    first = lax.broadcasted_iota(jnp.int32, (8, 256), 0) == 0
+    first = lax.broadcasted_iota(jnp.int32, (8, 128), 0) == 0
+    src = lax.broadcasted_iota(jnp.int32, (256, 256), 0)
+    dst = lax.broadcasted_iota(jnp.int32, (256, 256), 1)
+    for i in range(ROLLED, 8, 2):
+        moved = jnp.where(dst < 128, 128 + dst - 16 * i, dst - 16 * (i + 1))
+        shift_ref[(i - ROLLED) // 2] = jnp.where(src == moved, 1.0, 0.0).astype(BF16)
     for q in range(per_peer):
-        wide_ref[q, :, :128] = jnp.zeros((128, 128), BF16)
-        wide_ref[q, :, 34 * 128:] = jnp.zeros((128, 128), BF16)
+        wide_ref[q, 0] = jnp.zeros((128, 128), BF16)
+        wide_ref[q, 34] = jnp.zeros((128, 128), BF16)
 
     for q in range(per_peer):
-        before = [jnp.zeros((16, 128), BF16)] * 8
+        none = jnp.zeros((16, 128), BF16)
+        steep_ref[q, 0] = none
+        rolled = none
+        before = [none] * ROLLED
         for j in range(33):
             if j < 32:
                 line = jnp.broadcast_to(taps_ref[q, pl.ds(j, 1), :], (16, 128))
-                base = pltpu.roll(line, 0, 1, stride=1, stride_axis=0)
-                now = [pltpu.roll(base, 16 * i, 1).astype(BF16) if i else base.astype(BF16) for i in range(8)]
+                turned = pltpu.roll(line, 0, 1, stride=1, stride_axis=0).astype(BF16)
             else:
-                now = [jnp.zeros((16, 128), BF16)] * 8
-            for i in range(8):
-                wide_ref[q, pl.ds(16 * i, 16), pl.ds(128 * (j + 1), 128)] = jnp.where(
-                    lane >= sub + 16 * i, now[i], before[i]
-                )
-            before = now
-        tiles = []
-        for p in range(positions):
-            halves = []
-            for h in range(2):
+                turned = none
+            strip = jnp.where(lane >= sub, turned, rolled)
+            rolled = turned
+            steep_ref[q, j + 1] = strip
+            wide_ref[q, j + 1, pl.ds(0, 16), :] = strip
+            for i in range(1, ROLLED):
+                now = pltpu.roll(strip, 16 * i, 1)
+                wide_ref[q, j + 1, pl.ds(16 * i, 16), :] = jnp.where(lane >= 16 * i, now, before[i])
+                before[i] = now
+        lhs = jnp.concatenate(
+            [steep_ref[q, 0:33].reshape(33 * 16, 128), steep_ref[q, 1:34].reshape(33 * 16, 128)], axis=1
+        )
+        for i in range(ROLLED, 8, 2):
+            moved = jnp.dot(lhs, shift_ref[(i - ROLLED) // 2], preferred_element_type=F32).astype(BF16)
+            for n in range(2):
+                wide_ref[q, 1:34, pl.ds(16 * (i + n), 16), :] = moved[:, 128 * n:128 * n + 128].reshape(33, 16, 128)
+        for h in range(2):
+            tiles = []
+            for p in range(positions):
                 start = (p // 4) * chunk + q * 8 + (p % 4) * 2 + h
-                halves.append(flat_ref[pl.ds(start, 8, stride=pitch), :])
-            tiles.append(jnp.concatenate(halves, axis=1))
-        line = [jnp.where(first, 0.0, pltpu.roll(tiles[p + positions - LAGS], 1, 0)) for p in range(LAGS)] + tiles
-        for a in range(len(line) // 2):
-            even_ref[q, pl.ds(16 * a, 16), :] = jnp.concatenate([line[2 * a], line[2 * a + 1]], axis=0).astype(BF16)
-        for a in range(len(line) // 2 - 1):
-            odd_ref[q, pl.ds(16 * a, 16), :] = jnp.concatenate([line[2 * a + 1], line[2 * a + 2]], axis=0).astype(BF16)
+                tiles.append(flat_ref[pl.ds(start, 8, stride=pitch), :])
+            line = [jnp.where(first, 0.0, pltpu.roll(tiles[p + positions - LAGS], 1, 0)) for p in range(LAGS)] + tiles
+            for a in range(len(line) // 2):
+                even_ref[q, h, pl.ds(16 * a, 16), :] = jnp.concatenate([line[2 * a], line[2 * a + 1]], axis=0).astype(BF16)
+            for a in range(len(line) // 2 - 1):
+                odd_ref[q, h, pl.ds(16 * a, 16), :] = jnp.concatenate([line[2 * a + 1], line[2 * a + 2]], axis=0).astype(BF16)
         acc = None
         for s in range(LAGS + 1):
             start = LAGS - s
             if start % 2 == 0:
-                lhs = even_ref[q, pl.ds(start * 8, rows), :]
+                lhs = [even_ref[q, h, pl.ds(start * 8, rows), :] for h in range(2)]
             else:
-                lhs = odd_ref[q, pl.ds((start - 1) * 8, rows), :]
-            u = s * BLOCK
-            rhs = jnp.concatenate([wide_ref[q, :, u + 128:u + 384], wide_ref[q, :, u:u + 256]], axis=0)
+                lhs = [odd_ref[q, h, pl.ds((start - 1) * 8, rows), :] for h in range(2)]
+            lhs = jnp.concatenate(lhs, axis=1)
+            t = 2 * s
+            rhs = jnp.concatenate(
+                [
+                    jnp.concatenate([wide_ref[q, t + 1], wide_ref[q, t + 2]], axis=1),
+                    jnp.concatenate([wide_ref[q, t], wide_ref[q, t + 1]], axis=1),
+                ],
+                axis=0,
+            )
             term = jnp.dot(lhs, rhs, preferred_element_type=F32)
             acc = term if acc is None else acc + term
         mine = lax.broadcasted_iota(jnp.int32, (2, 128), 0) * 128 + lax.broadcasted_iota(jnp.int32, (2, 128), 1)
@@ -164,24 +187,28 @@
     square_ref[...] = total[:8] + total[8:]
 
 
-def norm_kernel(conv_ref, og_ref, square_ref, out_hbm, rows_ref, out_ref, sems):
-    rows = conv_ref.shape[0]
-    tokens, channels = out_ref.shape
-    count = tokens // 128
-    peers = rows // 32
+def mix_kernel(conv_ref, og_ref, mixed_ref, rows_ref):
+    peers = conv_ref.shape[0] // 32
+    count, channels, _ = mixed_ref.shape
     per_peer = channels // peers
-    power = (square_ref[0] + square_ref[1] + square_ref[2] + square_ref[3]) * (1.0 / CH)
+    for j in range(peers):
+        part = pl.ds(j * 32, 32)
+        rows_ref[pl.ds(j * 40, 32), :] = conv_ref[part, :].astype(F32) * og_ref[part, :].astype(F32)
+    for b in range(count):
+        for q in range(per_peer):
+            mixed_ref[b, pl.ds(q * peers, peers), :] = rows_ref[pl.ds(q * count + b, peers, stride=40), :]
+
+
+def norm_kernel(mixed_ref, own_ref, first_ref, second_ref, third_ref, out_hbm, out_ref, sems):
+    count = mixed_ref.shape[0]
+    power = (own_ref[...] + first_ref[...] + second_ref[...] + third_ref[...]) * (1.0 / CH)
     scale = 1.0 / jnp.sqrt(power + 1e-05)
-    scale = jnp.concatenate([scale, scale], axis=0)
-    for n in range(rows // 16):
-        part = pl.ds(n * 16, 16)
-        rows_ref[part, :] = conv_ref[part, :].astype(F32) * og_ref[part, :].astype(F32) * scale
     eye = identity(128)
     copies = []
     for b in range(count):
-        got = [rows_ref[pl.ds(q * count + b, peers, stride=32), :] for q in range(per_peer)]
         part = pl.ds(b * 128, 128)
-        out_ref[part, :] = flipped(eye, jnp.concatenate(got, axis=0).astype(BF16)).astype(BF16)
+        scaled = (mixed_ref[b] * scale[b:b + 1, :]).astype(BF16)
+        out_ref[part, :] = flipped(eye, scaled).astype(BF16)
         copies.append(pltpu.make_async_copy(out_ref.at[part], out_hbm.at[part], sems.at[b]))
         copies[-1].start()
     for copy in copies:
@@ -227,11 +254,13 @@
         in_specs=[VMEM, VMEM],
         out_specs=VMEM,
         scratch_shapes=[
-            pltpu.VMEM((SEGS * 280, 128), F32),
+            pltpu.VMEM((SEGS * 276, 128), F32),
             pltpu.VMEM((4, 32, 128), F32),
-            pltpu.VMEM((4, 384, 256), BF16),
-            pltpu.VMEM((4, 384, 256), BF16),
-            pltpu.VMEM((4, 128, 35 * 128), BF16),
+            pltpu.VMEM((4, 2, 384, 128), BF16),
+            pltpu.VMEM((4, 2, 384, 128), BF16),
+            pltpu.VMEM((4, 34, 16, 128), BF16),
+            pltpu.VMEM((4, 256, 256), BF16),
+            pltpu.VMEM((4, 35, 128, 128), BF16),
             pltpu.VMEM((4, 512, 128), F32),
         ],
         compiler_params=params(24),
@@ -248,20 +277,27 @@
         compiler_params=params(8),
         name="square",
     )(convolved, turned)
-    squares = lax.all_gather(squares, "mp")
+    group = lax.axis_size("mp")
+    others = [lax.ppermute(squares, "mp", [(i, (i + k) % group) for i in range(group)]) for k in range(1, group)]
+    mixed = pl.pallas_call(
+        mix_kernel,
+        out_shape=shape((count, channels, 128), F32),
+        in_specs=[VMEM] * 2,
+        out_specs=VMEM,
+        scratch_shapes=[pltpu.VMEM((peers * 40, 128), F32)],
+        compiler_params=params(8),
+        cost_estimate=pl.CostEstimate(flops=20000000, bytes_accessed=8 * tokens * channels, transcendentals=0),
+        name="mix",
+    )(convolved, turned)
     return pl.pallas_call(
         norm_kernel,
         out_shape=shape((tokens, channels), BF16),
-        in_specs=[VMEM] * 3,
+        in_specs=[VMEM] * 5,
         out_specs=HBM,
-        scratch_shapes=[
-            pltpu.VMEM((rows, 128), F32),
-            pltpu.VMEM((tokens, channels), BF16),
-            pltpu.SemaphoreType.DMA((count,)),
-        ],
-        compiler_params=params(12),
+        scratch_shapes=[pltpu.VMEM((tokens, channels), BF16), pltpu.SemaphoreType.DMA((count,))],
+        compiler_params=params(8),
         name="norm",
-    )(convolved, turned, squares)
+    )(mixed, squares, *others)
 
 
 def solution(mesh):

time: 75.2 us -> 70.6 us (0.939)
  blocking collectives: 65.2 us -> 56.3 us
  starting transfers between devices: 0 us -> 5.61 us
  Pallas kernels: 7.72 us -> 5.91 us
    all_gather x1 -> x0, blocking collectives: 8.83 us -> none  [local(): squares = lax.all_gather(squares, 'mp')]
    ppermute x0 -> x3, starting transfers between devices: none -> 5.61 us  [local(): lax.ppermute(squares, 'mp', [(i, (i + k) % group) for i in range(group)])]
    pallas_call x1, Pallas kernels: 4.88 us -> 3.33 us  [local(): pl.pallas_call(conv_kernel, out_shape=shape((rows, 128), BF16), in_specs=...]
  transfers between devices with their start and end apart: 0 -> 3, of which waited for: 0 -> 1; matrix products, arithmetic and copies ran while one was open for 0% -> 0% of each run, Pallas kernels for 0% -> 0%
where the time goes in v3:
time: 70.6 us; the launch traced here: 70.4 us
  blocking collectives  56.3 us (80%)
  Pallas kernels  5.91 us (8%)
  starting transfers between devices  5.61 us (8%)
  other arithmetic  1.39 us (2%)
    all_to_all x1, blocking collectives, local(): lax.all_to_all(message.reshape(peers, 17, 2, 128), 'seq', split_axis=0, c...  33.1 us
    all_to_all x1, blocking collectives, local(): lax.all_to_all(convolved.reshape(peers, 32, 128), 'seq', split_axis=0, co...  23.2 us
    ppermute x3, starting transfers between devices, local(): lax.ppermute(squares, 'mp', [(i, (i + k) % group) for i in range(group)])  5.61 us
    pallas_call x1, Pallas kernels, local(): pl.pallas_call(conv_kernel, out_shape=shape((rows, 128), BF16), in_specs=...  3.33 us
  transfers between devices with their start and end apart: 3, of which 1 were waited for; matrix products, arithmetic and copies ran while one was open for 0% of the time, Pallas kernels for 0%

profile of v3, /device:TPU:1, one launch (start us, length us, event | category | flops | bytes accessed | tf_op | source)
XLA Modules:
  0.0 70.4 jit_solution(3254670393534420319)
XLA Ops:
  0.0 0.0 copy-start.1
  0.0 0.0 copy-start
  0.0 1.4 %multiply_convert_fusion.gated_ref = bf16[1024,256]{1,0:T(8,128)(2,1)S(1)} fusion(bf16[1024,256]{1,0:T(8,128)(2,1)} %param.6, bf16[1024,256]{1,0:T(8,128)(2,1)} %param.5), kind=kLoop, calls=%fused_computation | loop fusion | flops 1048576 | bytes 1572864 | tf_op jit(solution)/shard_map/convert_element_type | solution.py:237
  1.4 0.0 copy-start.2
  1.4 0.0 copy-done.1
  1.4 0.0 copy-done
  1.4 0.7 copy-done.2
  2.1 1.0 %gate.1 = (bf16[2176,128]{1,0:T(8,128)(2,1)S(1)}, bf16[2048,128]{1,0:T(8,128)(2,1)S(1)}, f32[2,128]{1,0:T(2,128)S(1)}) custom-call(bf16[1024,256]{1,0:T(8,128)(2,1)S(1)} %multiply_convert_fusion.gated_ref, bf16[1024,256]{1,0:T(8,128)(2,1)S(1)} %copy-done, bf16[64,256]{1,0:T(8,128)(2,1)S(1)} %copy-done.1, f32[2,128]{1,0:T(2,128)S(1)} %bitcast.10), custom_call_target="tpu_custom_call" | custom-call | tf_op jit(solution)/shard_map/gate/pallas_call | solution.py:238
  3.1 33.1 %all_to_all.10 = bf16[64,17,2,128]{3,2,1,0:T(2,128)(2,1)S(1)} all-to-all(bf16[64,17,2,128]{3,2,1,0:T(2,128)(2,1)S(1)} %bitcast.9), channel_id=1, replica_groups=mesh['seq'=64,'mp'=4] {'seq'}, dimensions={0} | all-to-all | bytes 1114112 | tf_op jit(solution)/shard_map/all_to_all | solution.py:250
  36.2 3.3 %conv.1 = bf16[2048,128]{1,0:T(8,128)(2,1)S(1)} custom-call(f32[2,128]{1,0:T(2,128)S(1)} %get-tuple-element.8.skip_ref, bf16[2176,128]{1,0:T(8,128)(2,1)S(1)} %bitcast.7), custom_call_target="tpu_custom_call" | custom-call | tf_op jit(solution)/shard_map/conv/pallas_call | solution.py:251
  39.6 23.2 %all_to_all.11 = bf16[64,32,128]{2,1,0:T(8,128)(2,1)S(1)} all-to-all(bf16[64,32,128]{2,1,0:T(8,128)(2,1)S(1)} %bitcast.8), channel_id=1, replica_groups=mesh['seq'=64,'mp'=4] {'seq'}, dimensions={0} | all-to-all | bytes 1048576 | tf_op jit(solution)/shard_map/all_to_all | solution.py:269
  62.8 0.2 square.1.own_ref
  63.0 3.9 %collective-permute-start.2 = (f32[8,128]{1,0:T(8,128)S(1)}, f32[8,128]{1,0:T(8,128)S(1)}, u32[]{:S(2)}, u32[]{:S(2)}) collective-permute-start(f32[8,128]{1,0:T(8,128)S(1)} %square.1.own_ref), channel_id=1, source_target_pairs={{0,3},{1,0},{2,1},{3,2},{4,7},{5,4},{6,5},{7,6},{8,11},{9,8},{10,9... | collective-permute-start | bytes 12296 | tf_op jit(solution)/shard_map/ppermute | solution.py:281
  66.9 0.3 collective-permute-start.1
  67.2 1.4 %collective-permute-start = (f32[8,128]{1,0:T(8,128)S(1)}, f32[8,128]{1,0:T(8,128)S(1)}, u32[]{:S(2)}, u32[]{:S(2)}) collective-permute-start(f32[8,128]{1,0:T(8,128)S(1)} %square.1.own_ref), channel_id=1, source_target_pairs={{0,1},{1,2},{2,3},{3,0},{4,5},{5,6},{6,7},{7,4},{8,9},{9,10},{10,1... | collective-permute-start | bytes 12296 | tf_op jit(solution)/shard_map/ppermute | solution.py:281
  68.6 0.3 mix.1.mixed_ref
  68.9 0.0 collective-permute-done.2.third_ref
  68.9 0.4 collective-permute-done.1.second_ref
  69.3 0.0 collective-permute-done.first_ref
  69.4 1.1 %norm.1 = bf16[1024,256]{1,0:T(8,128)(2,1)} custom-call(f32[8,256,128]{2,1,0:T(8,128)S(1)} %mix.1.mixed_ref, f32[8,128]{1,0:T(8,128)S(1)} %square.1.own_ref, f32[8,128]{1,0:T(8,128)S(1)} %collective-permute-done.first_ref, f32[8,128]{1,0:T(8,128)S(1)} %collective-permute-done.1.second_ref, f32[8,128]{1,0:T(8,128)S(1)} %collective-permute-done.2.third_ref), custom_call_target="tpu_custom_call" | custom-call | tf_op jit(solution)/shard_map/norm/pallas_call | solution.py:292
Async XLA Ops:
  0.0 1.4 %copy-start.1 = (bf16[64,256]{1,0:T(8,128)(2,1)S(1)}, bf16[64,256]{1,0:T(8,128)(2,1)}, u32[]{:S(2)}) copy-start(bf16[64,256]{1,0:T(8,128)(2,1)} %taps_ref.1) | copy-start | bytes 98308
  0.0 1.4 %copy-start = (bf16[1024,256]{1,0:T(8,128)(2,1)S(1)}, bf16[1024,256]{1,0:T(8,128)(2,1)}, u32[]{:S(2)}) copy-start(bf16[1024,256]{1,0:T(8,128)(2,1)} %og_ref.1) | copy-start | bytes 1572868
  1.4 0.7 copy-start.2
  63.0 5.9 %collective-permute-start.2 = (f32[8,128]{1,0:T(8,128)S(1)}, f32[8,128]{1,0:T(8,128)S(1)}, u32[]{:S(2)}, u32[]{:S(2)}) collective-permute-start(f32[8,128]{1,0:T(8,128)S(1)} %square.1.own_ref), channel_id=1, source_target_pairs={{0,3},{1,0},{2,1},{3,2},{4,7},{5,4},{6,5},{7,6},{8,11},{9,8},{10,9... | collective-permute-start | bytes 12296 | tf_op jit(solution)/shard_map/ppermute | solution.py:281
  66.9 2.5 %collective-permute-start.1 = (f32[8,128]{1,0:T(8,128)S(1)}, f32[8,128]{1,0:T(8,128)S(1)}, u32[]{:S(2)}, u32[]{:S(2)}) collective-permute-start(f32[8,128]{1,0:T(8,128)S(1)} %square.1.own_ref), channel_id=1, source_target_pairs={{0,2},{1,3},{2,0},{3,1},{4,6},{5,7},{6,4},{7,5},{8,10},{9,11},{10,... | collective-permute-start | bytes 12296 | tf_op jit(solution)/shard_map/ppermute | solution.py:281
  67.2 2.2 %collective-permute-start = (f32[8,128]{1,0:T(8,128)S(1)}, f32[8,128]{1,0:T(8,128)S(1)}, u32[]{:S(2)}, u32[]{:S(2)}) collective-permute-start(f32[8,128]{1,0:T(8,128)S(1)} %square.1.own_ref), channel_id=1, source_target_pairs={{0,1},{1,2},{2,3},{3,0},{4,5},{5,6},{6,7},{7,4},{8,9},{9,10},{10,1... | collective-permute-start | bytes 12296 | tf_op jit(solution)/shard_map/ppermute | solution.py:281

commit v4 on v3

--- a/solution.py
+++ b/solution.py
@@ -27,29 +27,55 @@
     return lax.dot_general(eye, block, NT, preferred_element_type=F32)
 
 
-def gate_kernel(gated_ref, og_ref, taps_ref, skip_ref, out_ref, og_out_ref, skip_out_ref, rows_ref, og_rows_ref):
-    skip_out_ref[...] = skip_ref[...]
-    tokens, channels = gated_ref.shape
+def gate_kernel(gate_hbm, value_hbm, og_hbm, taps_hbm, skip_hbm, out_ref, og_out_ref, skip_out_ref,
+                gate_ref, value_ref, og_ref, taps_ref, rows_ref, og_rows_ref, sems):
+    tokens, channels = gate_ref.shape
     count = tokens // 128
     pitch = og_rows_ref.shape[0] // count
     chunk = 34
     peers = out_ref.shape[0] // chunk
     per_peer = channels // peers
+    step = 1024
+    fetch = []
+    for k in range(tokens // step):
+        part = pl.ds(k * step, step)
+        fetch.append([
+            pltpu.make_async_copy(src.at[part], dst.at[part], sems.at[n, k])
+            for n, (src, dst) in enumerate(((gate_hbm, gate_ref), (value_hbm, value_ref)))
+        ])
+    rest = [
+        pltpu.make_async_copy(taps_hbm, taps_ref, sems.at[2, 0]),
+        pltpu.make_async_copy(og_hbm, og_ref, sems.at[2, 1]),
+        pltpu.make_async_copy(skip_hbm, skip_out_ref, sems.at[2, 2]),
+    ]
+    for copy in rest + [c for pair in fetch for c in pair]:
+        copy.start()
     eye = identity(channels)
+    front = 8 * pitch
+    wide = (2 * count + 8) * pitch
+    for copy in rest:
+        copy.wait()
     turned = flipped(eye, taps_ref[...])
-    wide = (2 * count + 8) * pitch
     for r in range(2):
         rows_ref[pl.ds(wide + r * (peers + 8), peers), :] = jnp.concatenate(
             [turned[2 * r * peers:(2 * r + 1) * peers], turned[(2 * r + 1) * peers:(2 * r + 2) * peers]], axis=1
         )
-    front = 8 * pitch
     for b in range(0, count, 2):
-        turned = flipped(eye, gated_ref[pl.ds(b * 128, 256), :])
-        for n in range(2):
-            rows_ref[pl.ds(front + (b + n) * pitch, channels), :] = turned[:, n * 128:(n + 1) * 128]
         turned = flipped(eye, og_ref[pl.ds(b * 128, 256), :])
         for n in range(2):
             og_rows_ref[pl.ds((b + n) * pitch, channels), :] = turned[:, n * 128:(n + 1) * 128]
+    for j in range(peers):
+        got = [og_rows_ref[pl.ds(q * peers + j, count, stride=pitch), :] for q in range(per_peer)]
+        og_out_ref[pl.ds(j * 32, 32), :] = jnp.concatenate(got, axis=0).astype(BF16)
+    for k, pair in enumerate(fetch):
+        for copy in pair:
+            copy.wait()
+        part = pl.ds(k * step, step)
+        gated = (gate_ref[part, :].astype(F32) * value_ref[part, :].astype(F32)).astype(BF16)
+        for m in range(step // 256):
+            turned = flipped(eye, gated[m * 256:(m + 1) * 256])
+            for n in range(2):
+                rows_ref[pl.ds(front + ((step // 128) * k + 2 * m + n) * pitch, channels), :] = turned[:, n * 128:(n + 1) * 128]
     sub = lax.broadcasted_iota(jnp.int32, (8, 128), 0)
 
     def tile(first):
@@ -74,9 +100,6 @@
 
     for n in range(peers * chunk // 16):
         out_ref[pl.ds(n * 16, 16), :] = jnp.concatenate([tile(n * 16), tile(n * 16 + 8)], axis=0).astype(BF16)
-    for j in range(peers):
-        got = [og_rows_ref[pl.ds(q * peers + j, count, stride=pitch), :] for q in range(per_peer)]
-        og_out_ref[pl.ds(j * 32, 32), :] = jnp.concatenate(got, axis=0).astype(BF16)
 
 
 def conv_kernel(skip_ref, x_ref, out_ref, flat_ref, taps_ref, even_ref, odd_ref, steep_ref, shift_ref, wide_ref, out_rows):
@@ -234,19 +257,24 @@
     per_peer = channels // peers
     count = tokens // 128
     rows = peers * per_peer * count
-    gated = (gate_in.astype(F32) * value_in.astype(F32)).astype(BF16)
+    inputs = (gate_in, value_in, out_gate, filter_taps, skip_gain.reshape(channels // 128, 128))
     message, turned, skip = pl.pallas_call(
         gate_kernel,
         out_shape=(shape((peers * 34, 128), BF16), shape((rows, 128), BF16), shape((channels // 128, 128), F32)),
-        in_specs=[VMEM] * 4,
+        in_specs=[HBM] * 5,
         out_specs=(VMEM,) * 3,
         scratch_shapes=[
+            pltpu.VMEM((tokens, channels), BF16),
+            pltpu.VMEM((tokens, channels), BF16),
+            pltpu.VMEM((tokens, channels), BF16),
+            pltpu.VMEM(filter_taps.shape, BF16),
             pltpu.VMEM(((2 * count + 8) * (channels + 8) + 16 * (peers + 8), 128), F32),
             pltpu.VMEM((count * (channels + 8), 128), F32),
+            pltpu.SemaphoreType.DMA((3, tokens // 256)),
         ],
-        compiler_params=params(12),
+        compiler_params=params(16),
         name="gate",
-    )(gated, out_gate, filter_taps, skip_gain.reshape(channels // 128, 128))
+    )(*(pltpu.with_memory_space_constraint(a, pltpu.HBM) for a in inputs))
     message = lax.all_to_all(message.reshape(peers, 17, 2, 128), "seq", split_axis=0, concat_axis=0, tiled=True)
     convolved = pl.pallas_call(
         conv_kernel,

time: 70.6 us -> 69.7 us (0.987)
  other arithmetic: 1.39 us -> 0 us
  Pallas kernels: 5.91 us -> 7.11 us
    convert_element_type x1 -> x0, other arithmetic: 1.39 us -> none  [local(): gated = (gate_in.astype(F32) * value_in.astype(F32)).astype(BF16)]
    pallas_call x1, Pallas kernels: 1.02 us -> 2.22 us  [local(): pl.pallas_call(gate_kernel, out_shape=(shape((peers * 34, 128), BF16), sh...]
where the time goes in v4:
time: 69.7 us; the launch traced here: 69.5 us
  blocking collectives  56.3 us (81%)
  Pallas kernels  7.11 us (10%)
  starting transfers between devices  5.62 us (8%)
    all_to_all x1, blocking collectives, local(): lax.all_to_all(message.reshape(peers, 17, 2, 128), 'seq', split_axis=0, c...  33.1 us
    all_to_all x1, blocking collectives, local(): lax.all_to_all(convolved.reshape(peers, 32, 128), 'seq', split_axis=0, co...  23.2 us
    ppermute x3, starting transfers between devices, local(): lax.ppermute(squares, 'mp', [(i, (i + k) % group) for i in range(group)])  5.62 us
    pallas_call x1, Pallas kernels, local(): pl.pallas_call(conv_kernel, out_shape=shape((rows, 128), BF16), in_specs=...  3.33 us
    pallas_call x1, Pallas kernels, local(): pl.pallas_call(gate_kernel, out_shape=(shape((peers * 34, 128), BF16), sh...  2.22 us
  transfers between devices with their start and end apart: 3, of which 1 were waited for; matrix products, arithmetic and copies ran while one was open for 0% of the time, Pallas kernels for 0%

profile of v4, /device:TPU:1, one launch (start us, length us, event | category | flops | bytes accessed | tf_op | source)
XLA Modules:
  0.0 69.5 jit_solution(18201457933297819099)
XLA Ops:
  0.0 2.2 %gate.1 = (bf16[2176,128]{1,0:T(8,128)(2,1)S(1)}, bf16[2048,128]{1,0:T(8,128)(2,1)S(1)}, f32[2,128]{1,0:T(2,128)S(1)}) custom-call(bf16[1024,256]{1,0:T(8,128)(2,1)} %gate_hbm.1, bf16[1024,256]{1,0:T(8,128)(2,1)} %value_hbm.1, bf16[1024,256]{1,0:T(8,128)(2,1)} %og_hbm.1, bf16[64,256]{1,0:T(8,128)(2,1)} %taps_hbm.1, f32[2,128]{1,0:T(2,128)} %bitcast.10), custom_call_target="tpu_custom_call" | custom-call | tf_op jit(solution)/shard_map/gate/pallas_call | solution.py:261
  2.2 33.1 %all_to_all.10 = bf16[64,17,2,128]{3,2,1,0:T(2,128)(2,1)S(1)} all-to-all(bf16[64,17,2,128]{3,2,1,0:T(2,128)(2,1)S(1)} %bitcast.9), channel_id=1, replica_groups=mesh['seq'=64,'mp'=4] {'seq'}, dimensions={0} | all-to-all | bytes 1114112 | tf_op jit(solution)/shard_map/all_to_all | solution.py:278
  35.3 3.3 %conv.1 = bf16[2048,128]{1,0:T(8,128)(2,1)S(1)} custom-call(f32[2,128]{1,0:T(2,128)S(1)} %get-tuple-element.8.skip_ref, bf16[2176,128]{1,0:T(8,128)(2,1)S(1)} %bitcast.7), custom_call_target="tpu_custom_call" | custom-call | tf_op jit(solution)/shard_map/conv/pallas_call | solution.py:279
  38.7 23.2 %all_to_all.11 = bf16[64,32,128]{2,1,0:T(8,128)(2,1)S(1)} all-to-all(bf16[64,32,128]{2,1,0:T(8,128)(2,1)S(1)} %bitcast.8), channel_id=1, replica_groups=mesh['seq'=64,'mp'=4] {'seq'}, dimensions={0} | all-to-all | bytes 1048576 | tf_op jit(solution)/shard_map/all_to_all | solution.py:297
  61.9 0.2 square.1.own_ref
  62.1 3.9 %collective-permute-start.2 = (f32[8,128]{1,0:T(8,128)S(1)}, f32[8,128]{1,0:T(8,128)S(1)}, u32[]{:S(2)}, u32[]{:S(2)}) collective-permute-start(f32[8,128]{1,0:T(8,128)S(1)} %square.1.own_ref), channel_id=1, source_target_pairs={{0,3},{1,0},{2,1},{3,2},{4,7},{5,4},{6,5},{7,6},{8,11},{9,8},{10,9... | collective-permute-start | bytes 12296 | tf_op jit(solution)/shard_map/ppermute | solution.py:309
  66.0 0.3 collective-permute-start.1
  66.3 1.4 %collective-permute-start = (f32[8,128]{1,0:T(8,128)S(1)}, f32[8,128]{1,0:T(8,128)S(1)}, u32[]{:S(2)}, u32[]{:S(2)}) collective-permute-start(f32[8,128]{1,0:T(8,128)S(1)} %square.1.own_ref), channel_id=1, source_target_pairs={{0,1},{1,2},{2,3},{3,0},{4,5},{5,6},{6,7},{7,4},{8,9},{9,10},{10,1... | collective-permute-start | bytes 12296 | tf_op jit(solution)/shard_map/ppermute | solution.py:309
  67.7 0.3 mix.1.mixed_ref
  68.0 0.0 collective-permute-done.2.third_ref
  68.0 0.4 collective-permute-done.1.second_ref
  68.4 0.0 collective-permute-done.first_ref
  68.5 1.1 %norm.1 = bf16[1024,256]{1,0:T(8,128)(2,1)} custom-call(f32[8,256,128]{2,1,0:T(8,128)S(1)} %mix.1.mixed_ref, f32[8,128]{1,0:T(8,128)S(1)} %square.1.own_ref, f32[8,128]{1,0:T(8,128)S(1)} %collective-permute-done.first_ref, f32[8,128]{1,0:T(8,128)S(1)} %collective-permute-done.1.second_ref, f32[8,128]{1,0:T(8,128)S(1)} %collective-permute-done.2.third_ref), custom_call_target="tpu_custom_call" | custom-call | tf_op jit(solution)/shard_map/norm/pallas_call | solution.py:320
Async XLA Ops:
  62.1 5.9 %collective-permute-start.2 = (f32[8,128]{1,0:T(8,128)S(1)}, f32[8,128]{1,0:T(8,128)S(1)}, u32[]{:S(2)}, u32[]{:S(2)}) collective-permute-start(f32[8,128]{1,0:T(8,128)S(1)} %square.1.own_ref), channel_id=1, source_target_pairs={{0,3},{1,0},{2,1},{3,2},{4,7},{5,4},{6,5},{7,6},{8,11},{9,8},{10,9... | collective-permute-start | bytes 12296 | tf_op jit(solution)/shard_map/ppermute | solution.py:309
  66.0 2.5 %collective-permute-start.1 = (f32[8,128]{1,0:T(8,128)S(1)}, f32[8,128]{1,0:T(8,128)S(1)}, u32[]{:S(2)}, u32[]{:S(2)}) collective-permute-start(f32[8,128]{1,0:T(8,128)S(1)} %square.1.own_ref), channel_id=1, source_target_pairs={{0,2},{1,3},{2,0},{3,1},{4,6},{5,7},{6,4},{7,5},{8,10},{9,11},{10,... | collective-permute-start | bytes 12296 | tf_op jit(solution)/shard_map/ppermute | solution.py:309
  66.3 2.2 %collective-permute-start = (f32[8,128]{1,0:T(8,128)S(1)}, f32[8,128]{1,0:T(8,128)S(1)}, u32[]{:S(2)}, u32[]{:S(2)}) collective-permute-start(f32[8,128]{1,0:T(8,128)S(1)} %square.1.own_ref), channel_id=1, source_target_pairs={{0,1},{1,2},{2,3},{3,0},{4,5},{5,6},{6,7},{7,4},{8,9},{9,10},{10,1... | collective-permute-start | bytes 12296 | tf_op jit(solution)/shard_map/ppermute | solution.py:309

commit v5 on v4

--- a/solution.py
+++ b/solution.py
@@ -10,6 +10,7 @@
 BLOCK = 256
 LAGS = TAPS // BLOCK
 SEGS = 8
+STAGGER = 8000
 ROLLED = 6
 NT = (((1,), (1,)), ((), ()))
 F32 = jnp.float32
@@ -27,11 +28,11 @@
     return lax.dot_general(eye, block, NT, preferred_element_type=F32)
 
 
-def gate_kernel(gate_hbm, value_hbm, og_hbm, taps_hbm, skip_hbm, out_ref, og_out_ref, skip_out_ref,
-                gate_ref, value_ref, og_ref, taps_ref, rows_ref, og_rows_ref, sems):
+def gate_kernel(gate_hbm, value_hbm, taps_hbm, skip_hbm, og_hbm, out_ref, skip_out_ref, og_ref,
+                gate_ref, value_ref, taps_ref, rows_ref, sems):
     tokens, channels = gate_ref.shape
     count = tokens // 128
-    pitch = og_rows_ref.shape[0] // count
+    pitch = channels + 8
     chunk = 34
     peers = out_ref.shape[0] // chunk
     per_peer = channels // peers
@@ -48,25 +49,17 @@
         pltpu.make_async_copy(og_hbm, og_ref, sems.at[2, 1]),
         pltpu.make_async_copy(skip_hbm, skip_out_ref, sems.at[2, 2]),
     ]
-    for copy in rest + [c for pair in fetch for c in pair]:
+    for copy in rest[:1] + [c for pair in fetch for c in pair] + rest[1:]:
         copy.start()
     eye = identity(channels)
     front = 8 * pitch
     wide = (2 * count + 8) * pitch
-    for copy in rest:
-        copy.wait()
+    rest[0].wait()
     turned = flipped(eye, taps_ref[...])
     for r in range(2):
         rows_ref[pl.ds(wide + r * (peers + 8), peers), :] = jnp.concatenate(
             [turned[2 * r * peers:(2 * r + 1) * peers], turned[(2 * r + 1) * peers:(2 * r + 2) * peers]], axis=1
         )
-    for b in range(0, count, 2):
-        turned = flipped(eye, og_ref[pl.ds(b * 128, 256), :])
-        for n in range(2):
-            og_rows_ref[pl.ds((b + n) * pitch, channels), :] = turned[:, n * 128:(n + 1) * 128]
-    for j in range(peers):
-        got = [og_rows_ref[pl.ds(q * peers + j, count, stride=pitch), :] for q in range(per_peer)]
-        og_out_ref[pl.ds(j * 32, 32), :] = jnp.concatenate(got, axis=0).astype(BF16)
     for k, pair in enumerate(fetch):
         for copy in pair:
             copy.wait()
@@ -100,9 +93,15 @@
 
     for n in range(peers * chunk // 16):
         out_ref[pl.ds(n * 16, 16), :] = jnp.concatenate([tile(n * 16), tile(n * 16 + 8)], axis=0).astype(BF16)
-
-
-def conv_kernel(skip_ref, x_ref, out_ref, flat_ref, taps_ref, even_ref, odd_ref, steep_ref, shift_ref, wide_ref, out_rows):
+    for copy in rest[1:]:
+        copy.wait()
+
+    @pl.when(lax.rem(lax.axis_index("mp"), 2) == 1)
+    def _():
+        pl.delay(STAGGER)
+
+
+def conv_kernel(skip_ref, x_ref, og_ref, out_ref, og_out_ref, og_rows_ref, flat_ref, taps_ref, even_ref, odd_ref, steep_ref, shift_ref, wide_ref, out_rows):
     chunk = 34
     sources = x_ref.shape[0] // chunk
     per_peer = 4
@@ -131,7 +130,7 @@
         wide_ref[q, 0] = jnp.zeros((128, 128), BF16)
         wide_ref[q, 34] = jnp.zeros((128, 128), BF16)
 
-    for q in range(per_peer):
+    def toeplitz(q):
         none = jnp.zeros((16, 128), BF16)
         steep_ref[q, 0] = none
         rolled = none
@@ -157,6 +156,8 @@
             moved = jnp.dot(lhs, shift_ref[(i - ROLLED) // 2], preferred_element_type=F32).astype(BF16)
             for n in range(2):
                 wide_ref[q, 1:34, pl.ds(16 * (i + n), 16), :] = moved[:, 128 * n:128 * n + 128].reshape(33, 16, 128)
+
+    def signal(q):
         for h in range(2):
             tiles = []
             for p in range(positions):
@@ -167,6 +168,8 @@
                 even_ref[q, h, pl.ds(16 * a, 16), :] = jnp.concatenate([line[2 * a], line[2 * a + 1]], axis=0).astype(BF16)
             for a in range(len(line) // 2 - 1):
                 odd_ref[q, h, pl.ds(16 * a, 16), :] = jnp.concatenate([line[2 * a + 1], line[2 * a + 2]], axis=0).astype(BF16)
+
+    def multiply(q):
         acc = None
         for s in range(LAGS + 1):
             start = LAGS - s
@@ -193,6 +196,29 @@
                 start = (p // 4) * chunk + q * 8 + (p % 4) * 2 + h
                 own = flat_ref[pl.ds(start, 8, stride=pitch), :]
                 out_rows[q, pl.ds((p * 2 + h) * 8, 8), :] = acc[8 * p:8 * p + 8, h * 128:(h + 1) * 128] + skip * own
+    tokens, channels = og_ref.shape
+    count = tokens // 128
+    og_pitch = og_rows_ref.shape[0] // count
+    eye = identity(channels)
+    for b in range(0, count, 2):
+        turned = flipped(eye, og_ref[pl.ds(b * 128, 256), :])
+        for n in range(2):
+            og_rows_ref[pl.ds((b + n) * og_pitch, channels), :] = turned[:, n * 128:(n + 1) * 128]
+
+    def og_rows(first, last):
+        for j in range(first, last):
+            got = [og_rows_ref[pl.ds(q * sources + j, count, stride=og_pitch), :] for q in range(per_peer)]
+            og_out_ref[pl.ds(j * 32, 32), :] = jnp.concatenate(got, axis=0).astype(BF16)
+
+    toeplitz(0)
+    signal(0)
+    for q in range(per_peer):
+        og_rows(q * sources // per_peer, (q + 1) * sources // per_peer)
+        if q + 1 < per_peer:
+            toeplitz(q + 1)
+            signal(q + 1)
+        multiply(q)
+
     for j in range(sources):
         g, jj = divmod(j, per_seg)
         got = [out_rows[q, pl.ds(jj * 64 + g, 8, stride=8), :] for q in range(per_peer)]
@@ -257,31 +283,30 @@
     per_peer = channels // peers
     count = tokens // 128
     rows = peers * per_peer * count
-    inputs = (gate_in, value_in, out_gate, filter_taps, skip_gain.reshape(channels // 128, 128))
-    message, turned, skip = pl.pallas_call(
+    inputs = (gate_in, value_in, filter_taps, skip_gain.reshape(channels // 128, 128), out_gate)
+    message, skip, og_here = pl.pallas_call(
         gate_kernel,
-        out_shape=(shape((peers * 34, 128), BF16), shape((rows, 128), BF16), shape((channels // 128, 128), F32)),
+        out_shape=(shape((peers * 34, 128), BF16), shape((channels // 128, 128), F32), shape((tokens, channels), BF16)),
         in_specs=[HBM] * 5,
         out_specs=(VMEM,) * 3,
         scratch_shapes=[
             pltpu.VMEM((tokens, channels), BF16),
             pltpu.VMEM((tokens, channels), BF16),
-            pltpu.VMEM((tokens, channels), BF16),
             pltpu.VMEM(filter_taps.shape, BF16),
             pltpu.VMEM(((2 * count + 8) * (channels + 8) + 16 * (peers + 8), 128), F32),
-            pltpu.VMEM((count * (channels + 8), 128), F32),
             pltpu.SemaphoreType.DMA((3, tokens // 256)),
         ],
         compiler_params=params(16),
         name="gate",
     )(*(pltpu.with_memory_space_constraint(a, pltpu.HBM) for a in inputs))
     message = lax.all_to_all(message.reshape(peers, 17, 2, 128), "seq", split_axis=0, concat_axis=0, tiled=True)
-    convolved = pl.pallas_call(
+    convolved, turned = pl.pallas_call(
         conv_kernel,
-        out_shape=shape((rows, 128), BF16),
-        in_specs=[VMEM, VMEM],
-        out_specs=VMEM,
+        out_shape=(shape((rows, 128), BF16), shape((rows, 128), BF16)),
+        in_specs=[VMEM] * 3,
+        out_specs=(VMEM, VMEM),
         scratch_shapes=[
+            pltpu.VMEM((count * (channels + 8), 128), F32),
             pltpu.VMEM((SEGS * 276, 128), F32),
             pltpu.VMEM((4, 32, 128), F32),
             pltpu.VMEM((4, 2, 384, 128), BF16),
@@ -293,7 +318,7 @@
         ],
         compiler_params=params(24),
         name="conv",
-    )(skip, message.reshape(peers * 34, 128))
+    )(skip, message.reshape(peers * 34, 128), og_here)
     convolved = lax.all_to_all(
         convolved.reshape(peers, 32, 128), "seq", split_axis=0, concat_axis=0, tiled=True
     ).reshape(rows, 128)

time: 69.7 us -> 68 us (0.976); the launches traced: 69.5 us -> 66.8 us
  Pallas kernels: 7.11 us -> 15 us
  blocking collectives: 56.3 us -> 49 us
  starting transfers between devices: 5.62 us -> 2.41 us
    pallas_call x1, Pallas kernels: 2.22 us -> 9.93 us  [local(): pl.pallas_call(gate_kernel, out_shape=(shape((peers * 34, 128), BF16), sh...]
    all_to_all x1, blocking collectives: 33.1 us -> 29.2 us  [local(): lax.all_to_all(message.reshape(peers, 17, 2, 128), 'seq', split_axis=0, c...]
    all_to_all x1, blocking collectives: 23.2 us -> 19.7 us  [local(): lax.all_to_all(convolved.reshape(peers, 32, 128), 'seq', split_axis=0, co...]
    ppermute x3, starting transfers between devices: 5.62 us -> 2.41 us  [local(): lax.ppermute(squares, 'mp', [(i, (i + k) % group) for i in range(group)])]
  transfers between devices with their start and end apart: 3 -> 3, of which waited for: 1 -> 2; matrix products, arithmetic and copies ran while one was open for 0% -> 0% of each run, Pallas kernels for 0% -> 0%
where the time goes in v5:
time: 68 us; the launch traced here: 66.8 us
  blocking collectives  49 us (72%)
  Pallas kernels  15 us (22%)
  starting transfers between devices  2.41 us (4%)
    all_to_all x1, blocking collectives, local(): lax.all_to_all(message.reshape(peers, 17, 2, 128), 'seq', split_axis=0, c...  29.2 us
    all_to_all x1, blocking collectives, local(): lax.all_to_all(convolved.reshape(peers, 32, 128), 'seq', split_axis=0, co...  19.7 us
    pallas_call x1, Pallas kernels, local(): pl.pallas_call(gate_kernel, out_shape=(shape((peers * 34, 128), BF16), sh...  9.93 us
    pallas_call x1, Pallas kernels, local(): pl.pallas_call(conv_kernel, out_shape=(shape((rows, 128), BF16), shape((r...  3.49 us
    ppermute x3, starting transfers between devices, local(): lax.ppermute(squares, 'mp', [(i, (i + k) % group) for i in range(group)])  2.41 us
  transfers between devices with their start and end apart: 3, of which 2 were waited for; matrix products, arithmetic and copies ran while one was open for 0% of the time, Pallas kernels for 0%

profile of v5, /device:TPU:1, one launch (start us, length us, event | category | flops | bytes accessed | tf_op | source)
XLA Modules:
  0.0 66.8 jit_solution(3708058347008811404)
XLA Ops:
  0.0 9.9 %gate.1 = (bf16[2176,128]{1,0:T(8,128)(2,1)S(1)}, f32[2,128]{1,0:T(2,128)S(1)}, bf16[1024,256]{1,0:T(8,128)(2,1)S(1)}) custom-call(bf16[1024,256]{1,0:T(8,128)(2,1)} %gate_hbm.1, bf16[1024,256]{1,0:T(8,128)(2,1)} %value_hbm.1, bf16[64,256]{1,0:T(8,128)(2,1)} %taps_hbm.1, f32[2,128]{1,0:T(2,128)} %bitcast.10, bf16[1024,256]{1,0:T(8,128)(2,1)} %og_hbm.1), custom_call_target="tpu_custom_call" | custom-call | tf_op jit(solution)/shard_map/gate/pallas_call | solution.py:287
  9.9 29.2 %all_to_all.10 = bf16[64,17,2,128]{3,2,1,0:T(2,128)(2,1)S(1)} all-to-all(bf16[64,17,2,128]{3,2,1,0:T(2,128)(2,1)S(1)} %bitcast.8), channel_id=1, replica_groups=mesh['seq'=64,'mp'=4] {'seq'}, dimensions={0} | all-to-all | bytes 1114112 | tf_op jit(solution)/shard_map/all_to_all | solution.py:302
  39.2 3.5 %conv.1 = (bf16[2048,128]{1,0:T(8,128)(2,1)S(1)}, bf16[2048,128]{1,0:T(8,128)(2,1)S(1)}) custom-call(f32[2,128]{1,0:T(2,128)S(1)} %get-tuple-element.10.skip_ref, bf16[2176,128]{1,0:T(8,128)(2,1)S(1)} %bitcast.7, bf16[1024,256]{1,0:T(8,128)(2,1)S(1)} %get-tuple-element.12.og_ref), custom_call_target="tpu_custom_call" | custom-call | tf_op jit(solution)/shard_map/conv/pallas_call | solution.py:303
  42.7 19.7 %all_to_all.11 = bf16[64,32,128]{2,1,0:T(8,128)(2,1)S(1)} all-to-all(bf16[64,32,128]{2,1,0:T(8,128)(2,1)S(1)} %bitcast.9), channel_id=1, replica_groups=mesh['seq'=64,'mp'=4] {'seq'}, dimensions={0} | all-to-all | bytes 1048576 | tf_op jit(solution)/shard_map/all_to_all | solution.py:322
  62.4 0.2 square.1.own_ref
  62.6 0.1 collective-permute-start.2
  62.7 0.4 collective-permute-start.1
  63.1 1.9 %collective-permute-start = (f32[8,128]{1,0:T(8,128)S(1)}, f32[8,128]{1,0:T(8,128)S(1)}, u32[]{:S(2)}, u32[]{:S(2)}) collective-permute-start(f32[8,128]{1,0:T(8,128)S(1)} %square.1.own_ref), channel_id=1, source_target_pairs={{0,1},{1,2},{2,3},{3,0},{4,5},{5,6},{6,7},{7,4},{8,9},{9,10},{10,1... | collective-permute-start | bytes 12296 | tf_op jit(solution)/shard_map/ppermute | solution.py:334
  65.0 0.3 mix.1.mixed_ref
  65.3 0.4 collective-permute-done.2.third_ref
  65.7 0.0 collective-permute-done.1.second_ref
  65.7 0.1 collective-permute-done.first_ref
  65.8 1.1 %norm.1 = bf16[1024,256]{1,0:T(8,128)(2,1)} custom-call(f32[8,256,128]{2,1,0:T(8,128)S(1)} %mix.1.mixed_ref, f32[8,128]{1,0:T(8,128)S(1)} %square.1.own_ref, f32[8,128]{1,0:T(8,128)S(1)} %collective-permute-done.first_ref, f32[8,128]{1,0:T(8,128)S(1)} %collective-permute-done.1.second_ref, f32[8,128]{1,0:T(8,128)S(1)} %collective-permute-done.2.third_ref), custom_call_target="tpu_custom_call" | custom-call | tf_op jit(solution)/shard_map/norm/pallas_call | solution.py:345
Async XLA Ops:
  62.6 3.1 %collective-permute-start.2 = (f32[8,128]{1,0:T(8,128)S(1)}, f32[8,128]{1,0:T(8,128)S(1)}, u32[]{:S(2)}, u32[]{:S(2)}) collective-permute-start(f32[8,128]{1,0:T(8,128)S(1)} %square.1.own_ref), channel_id=1, source_target_pairs={{0,3},{1,0},{2,1},{3,2},{4,7},{5,4},{6,5},{7,6},{8,11},{9,8},{10,9... | collective-permute-start | bytes 12296 | tf_op jit(solution)/shard_map/ppermute | solution.py:334
  62.7 3.0 %collective-permute-start.1 = (f32[8,128]{1,0:T(8,128)S(1)}, f32[8,128]{1,0:T(8,128)S(1)}, u32[]{:S(2)}, u32[]{:S(2)}) collective-permute-start(f32[8,128]{1,0:T(8,128)S(1)} %square.1.own_ref), channel_id=1, source_target_pairs={{0,2},{1,3},{2,0},{3,1},{4,6},{5,7},{6,4},{7,5},{8,10},{9,11},{10,... | collective-permute-start | bytes 12296 | tf_op jit(solution)/shard_map/ppermute | solution.py:334
  63.1 2.7 %collective-permute-start = (f32[8,128]{1,0:T(8,128)S(1)}, f32[8,128]{1,0:T(8,128)S(1)}, u32[]{:S(2)}, u32[]{:S(2)}) collective-permute-start(f32[8,128]{1,0:T(8,128)S(1)} %square.1.own_ref), channel_id=1, source_target_pairs={{0,1},{1,2},{2,3},{3,0},{4,5},{5,6},{6,7},{7,4},{8,9},{9,10},{10,1... | collective-permute-start | bytes 12296 | tf_op jit(solution)/shard_map/ppermute | solution.py:334

commit v6 on v5

--- a/solution.py
+++ b/solution.py
@@ -11,7 +11,7 @@
 LAGS = TAPS // BLOCK
 SEGS = 8
 STAGGER = 8000
-ROLLED = 6
+ROLLED = (6, 6, 8, 8)
 NT = (((1,), (1,)), ((), ()))
 F32 = jnp.float32
 BF16 = jnp.bfloat16
@@ -123,18 +123,19 @@
     first = lax.broadcasted_iota(jnp.int32, (8, 128), 0) == 0
     src = lax.broadcasted_iota(jnp.int32, (256, 256), 0)
     dst = lax.broadcasted_iota(jnp.int32, (256, 256), 1)
-    for i in range(ROLLED, 8, 2):
+    for i in range(6, 8, 2):
         moved = jnp.where(dst < 128, 128 + dst - 16 * i, dst - 16 * (i + 1))
-        shift_ref[(i - ROLLED) // 2] = jnp.where(src == moved, 1.0, 0.0).astype(BF16)
+        shift_ref[(i - 6) // 2] = jnp.where(src == moved, 1.0, 0.0).astype(BF16)
     for q in range(per_peer):
         wide_ref[q, 0] = jnp.zeros((128, 128), BF16)
         wide_ref[q, 34] = jnp.zeros((128, 128), BF16)
 
     def toeplitz(q):
+        rolls = ROLLED[q]
         none = jnp.zeros((16, 128), BF16)
         steep_ref[q, 0] = none
         rolled = none
-        before = [none] * ROLLED
+        before = [none] * rolls
         for j in range(33):
             if j < 32:
                 line = jnp.broadcast_to(taps_ref[q, pl.ds(j, 1), :], (16, 128))
@@ -145,15 +146,15 @@
             rolled = turned
             steep_ref[q, j + 1] = strip
             wide_ref[q, j + 1, pl.ds(0, 16), :] = strip
-            for i in range(1, ROLLED):
+            for i in range(1, rolls):
                 now = pltpu.roll(strip, 16 * i, 1)
                 wide_ref[q, j + 1, pl.ds(16 * i, 16), :] = jnp.where(lane >= 16 * i, now, before[i])
                 before[i] = now
         lhs = jnp.concatenate(
             [steep_ref[q, 0:33].reshape(33 * 16, 128), steep_ref[q, 1:34].reshape(33 * 16, 128)], axis=1
         )
-        for i in range(ROLLED, 8, 2):
-            moved = jnp.dot(lhs, shift_ref[(i - ROLLED) // 2], preferred_element_type=F32).astype(BF16)
+        for i in range(rolls, 8, 2):
+            moved = jnp.dot(lhs, shift_ref[(i - 6) // 2], preferred_element_type=F32).astype(BF16)
             for n in range(2):
                 wide_ref[q, 1:34, pl.ds(16 * (i + n), 16), :] = moved[:, 128 * n:128 * n + 128].reshape(33, 16, 128)
 

time: 68 us -> 68 us (level)
  no operation moved by 1% of the time
where the time goes in v6:
time: 68 us; the launch traced here: 66.8 us
  blocking collectives  49 us (72%)
  Pallas kernels  14.9 us (22%)
  starting transfers between devices  2.41 us (4%)
    all_to_all x1, blocking collectives, local(): lax.all_to_all(message.reshape(peers, 17, 2, 128), 'seq', split_axis=0, c...  29.2 us
    all_to_all x1, blocking collectives, local(): lax.all_to_all(convolved.reshape(peers, 32, 128), 'seq', split_axis=0, co...  19.7 us
    pallas_call x1, Pallas kernels, local(): pl.pallas_call(gate_kernel, out_shape=(shape((peers * 34, 128), BF16), sh...  9.93 us
    pallas_call x1, Pallas kernels, local(): pl.pallas_call(conv_kernel, out_shape=(shape((rows, 128), BF16), shape((r...  3.45 us
    ppermute x3, starting transfers between devices, local(): lax.ppermute(squares, 'mp', [(i, (i + k) % group) for i in range(group)])  2.41 us
  transfers between devices with their start and end apart: 3, of which 2 were waited for; matrix products, arithmetic and copies ran while one was open for 0% of the time, Pallas kernels for 0%

profile of v6, /device:TPU:1, one launch (start us, length us, event | category | flops | bytes accessed | tf_op | source)
XLA Modules:
  0.0 66.8 jit_solution(10751771894668321577)
XLA Ops:
  0.0 9.9 %gate.1 = (bf16[2176,128]{1,0:T(8,128)(2,1)S(1)}, f32[2,128]{1,0:T(2,128)S(1)}, bf16[1024,256]{1,0:T(8,128)(2,1)S(1)}) custom-call(bf16[1024,256]{1,0:T(8,128)(2,1)} %gate_hbm.1, bf16[1024,256]{1,0:T(8,128)(2,1)} %value_hbm.1, bf16[64,256]{1,0:T(8,128)(2,1)} %taps_hbm.1, f32[2,128]{1,0:T(2,128)} %bitcast.10, bf16[1024,256]{1,0:T(8,128)(2,1)} %og_hbm.1), custom_call_target="tpu_custom_call" | custom-call | tf_op jit(solution)/shard_map/gate/pallas_call | solution.py:288
  9.9 29.2 %all_to_all.10 = bf16[64,17,2,128]{3,2,1,0:T(2,128)(2,1)S(1)} all-to-all(bf16[64,17,2,128]{3,2,1,0:T(2,128)(2,1)S(1)} %bitcast.8), channel_id=1, replica_groups=mesh['seq'=64,'mp'=4] {'seq'}, dimensions={0} | all-to-all | bytes 1114112 | tf_op jit(solution)/shard_map/all_to_all | solution.py:303
  39.2 3.5 %conv.1 = (bf16[2048,128]{1,0:T(8,128)(2,1)S(1)}, bf16[2048,128]{1,0:T(8,128)(2,1)S(1)}) custom-call(f32[2,128]{1,0:T(2,128)S(1)} %get-tuple-element.10.skip_ref, bf16[2176,128]{1,0:T(8,128)(2,1)S(1)} %bitcast.7, bf16[1024,256]{1,0:T(8,128)(2,1)S(1)} %get-tuple-element.12.og_ref), custom_call_target="tpu_custom_call" | custom-call | tf_op jit(solution)/shard_map/conv/pallas_call | solution.py:304
  42.6 19.7 %all_to_all.11 = bf16[64,32,128]{2,1,0:T(8,128)(2,1)S(1)} all-to-all(bf16[64,32,128]{2,1,0:T(8,128)(2,1)S(1)} %bitcast.9), channel_id=1, replica_groups=mesh['seq'=64,'mp'=4] {'seq'}, dimensions={0} | all-to-all | bytes 1048576 | tf_op jit(solution)/shard_map/all_to_all | solution.py:323
  62.4 0.2 square.1.own_ref
  62.6 0.1 collective-permute-start.2
  62.6 0.4 collective-permute-start.1
  63.0 1.9 %collective-permute-start = (f32[8,128]{1,0:T(8,128)S(1)}, f32[8,128]{1,0:T(8,128)S(1)}, u32[]{:S(2)}, u32[]{:S(2)}) collective-permute-start(f32[8,128]{1,0:T(8,128)S(1)} %square.1.own_ref), channel_id=1, source_target_pairs={{0,1},{1,2},{2,3},{3,0},{4,5},{5,6},{6,7},{7,4},{8,9},{9,10},{10,1... | collective-permute-start | bytes 12296 | tf_op jit(solution)/shard_map/ppermute | solution.py:335
  65.0 0.3 mix.1.mixed_ref
  65.3 0.4 collective-permute-done.2.third_ref
  65.7 0.0 collective-permute-done.1.second_ref
  65.7 0.1 collective-permute-done.first_ref
  65.7 1.1 %norm.1 = bf16[1024,256]{1,0:T(8,128)(2,1)} custom-call(f32[8,256,128]{2,1,0:T(8,128)S(1)} %mix.1.mixed_ref, f32[8,128]{1,0:T(8,128)S(1)} %square.1.own_ref, f32[8,128]{1,0:T(8,128)S(1)} %collective-permute-done.first_ref, f32[8,128]{1,0:T(8,128)S(1)} %collective-permute-done.1.second_ref, f32[8,128]{1,0:T(8,128)S(1)} %collective-permute-done.2.third_ref), custom_call_target="tpu_custom_call" | custom-call | tf_op jit(solution)/shard_map/norm/pallas_call | solution.py:346
Async XLA Ops:
  62.6 3.1 %collective-permute-start.2 = (f32[8,128]{1,0:T(8,128)S(1)}, f32[8,128]{1,0:T(8,128)S(1)}, u32[]{:S(2)}, u32[]{:S(2)}) collective-permute-start(f32[8,128]{1,0:T(8,128)S(1)} %square.1.own_ref), channel_id=1, source_target_pairs={{0,3},{1,0},{2,1},{3,2},{4,7},{5,4},{6,5},{7,6},{8,11},{9,8},{10,9... | collective-permute-start | bytes 12296 | tf_op jit(solution)/shard_map/ppermute | solution.py:335
  62.6 3.0 %collective-permute-start.1 = (f32[8,128]{1,0:T(8,128)S(1)}, f32[8,128]{1,0:T(8,128)S(1)}, u32[]{:S(2)}, u32[]{:S(2)}) collective-permute-start(f32[8,128]{1,0:T(8,128)S(1)} %square.1.own_ref), channel_id=1, source_target_pairs={{0,2},{1,3},{2,0},{3,1},{4,6},{5,7},{6,4},{7,5},{8,10},{9,11},{10,... | collective-permute-start | bytes 12296 | tf_op jit(solution)/shard_map/ppermute | solution.py:335
  63.0 2.7 %collective-permute-start = (f32[8,128]{1,0:T(8,128)S(1)}, f32[8,128]{1,0:T(8,128)S(1)}, u32[]{:S(2)}, u32[]{:S(2)}) collective-permute-start(f32[8,128]{1,0:T(8,128)S(1)} %square.1.own_ref), channel_id=1, source_target_pairs={{0,1},{1,2},{2,3},{3,0},{4,5},{5,6},{6,7},{7,4},{8,9},{9,10},{10,1... | collective-permute-start | bytes 12296 | tf_op jit(solution)/shard_map/ppermute | solution.py:335
